TPU v7x, 128 devices: a whole 4x4x4 slice. The times are simulated.
128 devices in a mesh: band: 16 (over z, y), chan: 4 (over x), member: 2 (over core).
Axes of the slice: x: 4, y: 4, z: 4, core: 2. Of those that a mesh axis runs over, the one named last changes fastest.
Arguments:
- noisy_state: bfloat16 [8, 84, 32768], P(('chan', 'member'), None, 'band'), may hold values from -6 to 6
- target_state: bfloat16 [8, 84, 32768], P(('chan', 'member'), None, 'band'), may hold values from -6 to 6
- noise_level: float32 [8], P(('chan', 'member')), may hold values from 0.3 to 3
- var_weight: float32 [84], replicated, may hold values from 0.3 to 3
- embed_in: bfloat16 [84, 512], replicated, may hold values from -0.625 to 0.625
- embed_out: bfloat16 [512, 512], replicated, may hold values from -0.25 to 0.25
- norm_gain: float32 [512], replicated, may hold values from 0.1 to 1.9
- qkv_weight: bfloat16 [3, 512, 512], replicated, may hold values from -0.25 to 0.25
- head_scale: float32 [4], replicated, may hold values from 1 to 4
- out_weight: bfloat16 [512, 512], replicated, may hold values from -0.25 to 0.25
- dec_weight: bfloat16 [512, 84], replicated, may hold values from -0.25 to 0.25
- g2m_node: int32 [32768], P('band'), may hold values from 0 to 8191, as said below
- m2g_node: int32 [32768], P('band'), may hold values from 0 to 8191, as said below
- neighbours: int32 [8192, 32], P('band'), may hold values from 0 to 8191, as said below
Outputs:
- loss_value: float32 [], replicated
- grad_dec: float32 [512, 84], replicated
- grad_out: float32 [512, 512], replicated
- grad_value: float32 [512, 512], replicated
Inputs may be any that keep to these rules, and one draw needn't show every extreme that they name: `g2m_node`: the node of cell g lies in patch g // 2048 or in a patch next to it; patch p holds the nodes p * 512 to (p + 1) * 512 - 1. `m2g_node`: the node of cell g lies in patch g // 2048 or in a patch next to it; patch p holds the nodes p * 512 to (p + 1) * 512 - 1. The neighbours of node n lie in patch n // 512 or in a patch next to it.
All inputs are finite; a program needn't handle non-finite values.
Results may differ from a plain program's by a relative error of at most 0.0003.
Values may be sent and summed in bfloat16 or wider, within the bound.
A program may use at most 64 MiB of HBM per device.

v0:
```python
import math

import jax
import jax.numpy as jnp
from jax import lax
from jax.sharding import PartitionSpec as P

D = 512
VARS = 84
HEADS = 4
G_DEV = 2048
M_DEV = 512
MEM_DEV = 1
HEAD_DIM = 128


def with_halo(array, sides, width):
    for axis, dim in sides:
        size, length = (lax.axis_size(axis), array.shape[dim])
        up = [(i, (i + 1) % size) for i in range(size - 1)]
        down = [(j, i) for i, j in up]
        last = lax.slice_in_dim(array, length - width, length, axis=dim)
        leading = lax.slice_in_dim(array, 0, width, axis=dim)
        before = lax.ppermute(last, axis, up)
        after = lax.ppermute(leading, axis, down)
        array = jnp.concatenate([before, array, after], axis=dim)
    return array


def rim_parts(partial_value, rows_patch):
    return jnp.concatenate([partial_value[:rows_patch], partial_value[2 * rows_patch :]], axis=0)


def with_rims(partial_value, grown, rows_patch):
    return partial_value[rows_patch : 2 * rows_patch] + grown[:rows_patch] + grown[3 * rows_patch :]


def unit_rows(values):
    return values * lax.rsqrt(jnp.mean(values * values, axis=-1, keepdims=True) + 1e-06)


def split_parts(values, count):
    pieces = []
    rest = values
    for index in range(count):
        piece = lax.optimization_barrier(rest.astype(jnp.bfloat16))
        pieces.append(piece)
        rest = rest - piece.astype(jnp.float32)
    return pieces


def split_einsum(form, left, right_values, count):
    total = None
    for piece in split_parts(right_values, count):
        term = jnp.einsum(form, left, piece, preferred_element_type=jnp.float32)
        total = term if total is None else total + term
    return total


def local(
    noisy_state,
    target_state,
    noise_level,
    var_weight,
    embed_in,
    embed_out,
    norm_gain,
    qkv_weight,
    head_scale,
    out_weight,
    dec_weight,
    g2m_node,
    m2g_node,
    neighbours,
):
    band_index = lax.axis_index("band")
    band_count = lax.axis_size("band")
    members_all = MEM_DEV * lax.axis_size("chan") * lax.axis_size("member")
    base_node = (band_index - 1) * M_DEV
    scale_all = 1.0 / (members_all * VARS)
    level_sq = noise_level * noise_level + 1.0
    scale_in = lax.rsqrt(level_sq)
    skip_scale = 1.0 / level_sq
    out_scale = noise_level * scale_in
    node_ids = jnp.arange(3 * M_DEV, dtype=jnp.int32)
    projected = jnp.einsum("mvg,vd->gmd", noisy_state, embed_in, preferred_element_type=jnp.float32)
    hidden = jax.nn.silu(scale_in[None, :, None] * projected).astype(jnp.bfloat16)
    enc_table = ((g2m_node - base_node)[:, None] == node_ids[None, :]).astype(jnp.bfloat16)
    node_hidden = jnp.einsum("gp,gmd->pmd", enc_table, hidden, preferred_element_type=jnp.float32)
    enc_part = split_einsum("de,pmd->pme", embed_out, node_hidden, 3)
    enc_grown = with_halo(rim_parts(enc_part, M_DEV), (("band", 0),), M_DEV)
    mesh_in = with_rims(enc_part, enc_grown, M_DEV)
    mean_sq = jnp.mean(mesh_in * mesh_in, axis=-1, keepdims=True)
    normed = (mesh_in * lax.rsqrt(mean_sq + 1e-05) * norm_gain).astype(jnp.bfloat16)
    queries = unit_rows(
        jnp.einsum(
            "nmd,de->nme", normed, qkv_weight[0], preferred_element_type=jnp.float32
        ).reshape(M_DEV, MEM_DEV, HEADS, HEAD_DIM)
    ).astype(jnp.bfloat16)
    wider = with_halo(normed, (("band", 0),), M_DEV)
    pair = jnp.einsum(
        "nmd,tde->tnme", wider, qkv_weight[1:], preferred_element_type=jnp.float32
    ).reshape(2, 3 * M_DEV, MEM_DEV, HEADS, HEAD_DIM)
    nearby = jnp.stack([unit_rows(pair[0]).astype(jnp.bfloat16), pair[1].astype(jnp.bfloat16)])
    local_nbrs = neighbours - base_node
    block_rows = math.gcd(M_DEV, max(8, 512 // MEM_DEV))
    block_count = M_DEV // block_rows

    def block_weights():
        scores = (
            jnp.einsum("nmhe,pmhe->nmhp", queries, nearby[0], preferred_element_type=jnp.float32)
            * (head_scale / HEAD_DIM)[None, None, :, None]
        )
        counts = jnp.sum(
            (local_nbrs[:, :, None] == node_ids[None, None, :]).astype(jnp.float32), axis=1
        )[:, None, None, :]
        exps = jnp.exp(scores)
        attn_probs = (exps / jnp.sum(counts * exps, axis=-1, keepdims=True)).astype(jnp.bfloat16)
        return counts * attn_probs.astype(jnp.float32)

    def attend(block_index):
        weights = block_weights()
        mixed_rows = None
        for piece in split_parts(weights, 2):
            term = jnp.einsum(
                "nmhp,pmhe->nmhe", piece, nearby[1], preferred_element_type=jnp.float32
            )
            mixed_rows = term if mixed_rows is None else mixed_rows + term
        return mixed_rows.astype(jnp.bfloat16)

    mixed_blocks = lax.map(attend, jnp.arange(block_count))
    attended = mixed_blocks.reshape(M_DEV, MEM_DEV, D)
    mesh_out = (
        mesh_in
        + jnp.einsum("nmd,de->nme", attended, out_weight, preferred_element_type=jnp.float32)
    ).astype(jnp.bfloat16)
    dec_table = ((m2g_node - base_node)[:, None] == node_ids[None, :]).astype(jnp.bfloat16)
    node_vars = jnp.einsum("nmc,cv->nmv", mesh_out, dec_weight, preferred_element_type=jnp.float32)
    vars_wide = with_halo(node_vars, (("band", 0),), M_DEV)
    net_full = split_einsum("gp,pmv->mvg", dec_table, vars_wide, 3)
    positions = (band_index * G_DEV + jnp.arange(G_DEV)).astype(jnp.float32)
    lat_weight = 0.2 + jnp.cos(math.pi * (positions + 0.5) / (G_DEV * band_count) - 0.5 * math.pi)
    weights_all = var_weight[:, None] * lat_weight[None, :]
    errors = (
        skip_scale[:, None, None] * noisy_state.astype(jnp.float32)
        + out_scale[:, None, None] * net_full
        - target_state.astype(jnp.float32)
    )
    loss_part = jnp.sum(weights_all * errors * errors) * scale_all
    grad_net = ((2.0 * out_scale * scale_all)[:, None, None] * weights_all * errors).astype(
        jnp.bfloat16
    )
    node_part = jnp.einsum("gp,mvg->pmv", dec_table, grad_net, preferred_element_type=jnp.float32)
    node_grown = with_halo(
        rim_parts(node_part, M_DEV).astype(jnp.bfloat16), (("band", 0),), M_DEV
    ).astype(jnp.float32)
    node_grad = with_rims(node_part, node_grown, M_DEV)
    grad_dec = jnp.einsum(
        "nmc,nmv->cv", mesh_out.astype(jnp.float32), node_grad, precision=lax.Precision.HIGHEST
    )
    mesh_grad = jnp.einsum(
        "nmv,cv->nmc", node_grad, dec_weight.astype(jnp.float32), precision=lax.Precision.HIGHEST
    ).astype(jnp.bfloat16)
    grad_out = jnp.einsum("nmd,nmc->dc", attended, mesh_grad, preferred_element_type=jnp.float32)
    head_grad = jnp.einsum(
        "nmc,dc->nmd", mesh_grad, out_weight, preferred_element_type=jnp.float32
    ).astype(jnp.bfloat16)
    head_grad = head_grad.reshape(M_DEV, MEM_DEV, HEADS, HEAD_DIM)

    def spread(carry, block_index):
        weights = block_weights()
        for piece in split_parts(weights, 2):
            carry = carry + jnp.einsum(
                "nmhp,nmhe->pmhe", piece, head_grad, preferred_element_type=jnp.float32
            )
        return (carry, None)

    empty_sums = jnp.zeros((3 * M_DEV, MEM_DEV, HEADS, HEAD_DIM), jnp.float32)
    value_part, unused_out = lax.scan(spread, empty_sums, jnp.arange(block_count))
    value_part = value_part.reshape(3 * M_DEV, MEM_DEV, D)
    value_grown = with_halo(
        rim_parts(value_part, M_DEV).astype(jnp.bfloat16), (("band", 0),), M_DEV
    ).astype(jnp.float32)
    value_grad = with_rims(value_part, value_grown, M_DEV).astype(jnp.bfloat16)
    grad_value = jnp.einsum("nmd,nmc->dc", normed, value_grad, preferred_element_type=jnp.float32)
    totals = lax.psum((loss_part, grad_dec, grad_out, grad_value), ("band", "chan", "member"))
    loss_value = totals[0] / (G_DEV * band_count)
    return (loss_value, totals[1], totals[2], totals[3])


def solution(mesh):
    in_specs = (
        P(("chan", "member"), None, "band"),
        P(("chan", "member"), None, "band"),
        P(("chan", "member")),
        P(),
        P(),
        P(),
        P(),
        P(),
        P(),
        P(),
        P(),
        P("band"),
        P("band"),
        P("band", None),
    )
    out_specs = (P(), P(), P(), P())
    return jax.shard_map(local, mesh=mesh, in_specs=in_specs, out_specs=out_specs, check_vma=False)
```

profile of v0, /device:TPU:1, one launch (start us, length us, event | category | flops | bytes accessed | tf_op | source)
XLA Modules:
  0.0 352.7 jit_solution(2971836261392929375)
XLA Ops:
  8.0 0.7 broadcast_subtract_fusion.2
  8.7 7.4 %fusion.9 = f32[1536,512]{1,0:T(8,128)} fusion(s32[2048]{0:T(1024)S(1)} %broadcast_subtract_fusion.2, bf16[84,512]{1,0:T(8,128)(2,1)} %param.18, f32[]{:T(128)} %bitcast.2, bf16[1,84,2048]{2,1,0:T(8,128)(2,1)} %param.14), kind=kOutput, calls=%fused_computation.18 | convolution fusion | flops 3409969152 | bytes 3584004 | tf_op jit(solution)/shard_map/gp,gmd->pmd/dot_general | solution.py:89
  16.1 2.2 convert_bitcast_fusion
  18.3 0.6 copy-done.2
  18.9 0.5 fusion.41
  19.5 0.7 subtract_convert_fusion.1
  20.1 1.0 fusion.49
  21.1 1.0 convolution_add_fusion.1
  22.1 1.0 convolution_add_fusion
  23.2 1.7 copy-done.4
  24.8 1.1 slice_bitcast_fusion.1
  26.0 4.1 %collective-permute-start = (f32[512,1,512]{2,0,1:T(8,128)}, f32[512,1,512]{2,0,1:T(8,128)S(1)}, u32[]{:S(2)}, u32[]{:S(2)}) collective-permute-start(f32[512,1,512]{2,0,1:T(8,128)} %get-tuple-element.53), channel_id=1, source_target_pairs={{0,8},{8,16},{16,24},{24,32},{32,40},{40,48},{48,56},{56,64},{64,7... | collective-permute-start | bytes 3145736 | tf_op jit(solution)/shard_map/ppermute | solution.py:24
  30.1 1.3 collective-permute-start.1
  31.6 43.2 %convert_reduce_fusion = f32[512,1536]{1,0:T(8,128)} fusion(s32[512,32]{1,0:T(8,128)S(1)} %copy.27), kind=kLoop, calls=%fused_computation | loop fusion | flops 74711040 | bytes 3211264 | tf_op jit(solution)/shard_map/while/body/eval_jaxpr/reduce_sum | solution.py:114
  74.8 1.5 multiply_reduce_fusion
  76.2 1.2 multiply_convert_fusion.3
  77.4 1.3 collective-permute-start.3
  78.7 5.4 %collective-permute-start.2 = (bf16[512,1,512]{2,0,1:T(8,128)(2,1)}, bf16[512,1,512]{2,0,1:T(8,128)(2,1)}, u32[]{:S(2)}, u32[]{:S(2)}) collective-permute-start(bf16[512,1,512]{2,0,1:T(8,128)(2,1)} %multiply_convert_fusion.3), channel_id=1, source_target_pairs={{0,8},{8,16},{16,24},{24,32},{32,40},{40,48},{48,56},{56,64},{64,7... | collective-permute-start | bytes 1572872 | tf_op jit(solution)/shard_map/ppermute | solution.py:24
  84.3 2.4 copy.28
  86.6 2.7 bitcast_reduce_fusion
  89.3 2.6 copy.30
  91.9 0.9 collective-permute-done.3
  92.8 0.9 collective-permute-done.2
  93.7 3.5 %convolution_bitcast_fusion = f32[2,1536,1,512]{1,3,0,2:T(8,128)S(1)} fusion(bf16[512,1,512]{2,0,1:T(8,128)(2,1)} %collective-permute-done.3, bf16[512,1,512]{2,0,1:T(8,128)(2,1)} %multiply_convert_fusion.3, bf16[512,1,512]{2,0,1:T(8,128)(2,1)} %collective-permute-done.2, bf16[3,512,512]{2,1,0:T(8,128)(2,1)} %param.21), kind=kOutput, calls=%fused_computation.32 | convolution fusion | flops 1615331328 | bytes 8912896 | tf_op jit(solution)/shard_map/nmd,tde->tnme/dot_general | solution.py:101
  97.2 1.3 slice.134
  98.5 3.6 %slice_multiply_fusion = (f32[1,1536,1,512]{1,3,0,2:T(8,128)}, f32[1,1536,1,512]{1,3,0,2:T(8,128)}) fusion(f32[2,1536,1,512]{1,3,0,2:T(8,128)S(1)} %convolution_bitcast_fusion), kind=kLoop, calls=%fused_computation.140 | loop fusion | flops 786432 | bytes 9437184 | tf_op jit(solution)/shard_map/mul | solution.py:39
  102.1 2.1 reduce_sum.68
  104.3 3.6 %copy.29 = f32[1536,4,128]{2,0,1:T(8,128)} copy(f32[1536,4,128]{0,2,1:T(8,128)} %bitcast.215) | data formatting | bytes 6291456 | tf_op jit(solution)/shard_map/squeeze | solution.py:104
  107.8 5.2 %fusion = (f32[512,4]{0,1:T(4,128)S(1)}, f32[4,1536,512]{2,1,0:T(8,128)S(1)}) fusion(f32[4]{0:T(128)S(1)} %broadcast_multiply_fusion, f32[512,1536]{0,1:T(8,128)S(1)} %copy.28, f32[512,4,128]{2,0,1:T(8,128)} %copy.30, f32[512,4]{0,1:T(4,128)S(1)} %add_rsqrt_fusion.1, f32[1536,4,128]{2,0,1:T(8,128)} %copy.29, f32[1536,4]{0,1:T(4,128)S(1)} %add_rsqrt_fusion), kind=kOutput, calls=%fused_computation.4 | convolution fusion | flops 816838656 | bytes 19963920 | tf_op jit(solution)/shard_map/while/body/eval_jaxpr/nmhe,pmhe->nmhp/dot_general | solution.py:111
  113.0 2.6 fusion.7
  115.6 3.6 %subtract_convert_fusion = bf16[512,1,4,1536]{0,3,2,1:T(8,128)(2,1)S(1)} fusion(bf16[512,1,4,1536]{0,3,2,1:T(8,128)(2,1)S(1)} %fusion.7, f32[512,1536]{0,1:T(8,128)S(1)} %copy.28, f32[512,4]{0,1:T(4,128)S(1)} %get-tuple-element.67, f32[4]{0:T(128)S(1)} %broadcast_multiply_fusion, f32[4,1536,512]{2,1,0:T(8,128)S(1)} %get-tuple-element.68), kind=kLoop, calls=%fused_computation.13 | loop fusion | flops 25165824 | bytes 28319760 | tf_op jit(solution)/shard_map/while/body/eval_jaxpr/convert_element_type | solution.py:46
  119.2 1.0 fusion.13
  120.3 1.0 fusion.57
  121.3 0.2 copy-done.6
  121.6 0.5 fusion.60
  122.1 0.3 convolution_bitcast_fusion.2
  122.3 1.3 collective-permute-start.5
  123.6 5.0 %collective-permute-start.4 = (f32[512,1,84]{0,2,1:T(8,128)S(1)}, f32[512,1,84]{0,2,1:T(8,128)S(1)}, u32[]{:S(2)}, u32[]{:S(2)}) collective-permute-start(f32[512,1,84]{0,2,1:T(8,128)S(1)} %convolution_bitcast_fusion.2), channel_id=1, source_target_pairs={{0,8},{8,16},{16,24},{24,32},{32,40},{40,48},{48,56},{56,64},{64,7... | collective-permute-start | bytes 516104 | tf_op jit(solution)/shard_map/ppermute | solution.py:24
  128.6 0.7 collective-permute-done.5
  129.3 1.5 collective-permute-done.4
  131.0 2.9 fusion.5
  133.9 3.0 fusion.35
  136.9 3.4 fusion.68
  140.3 2.6 fusion.3
  143.0 1.3 collective-permute-start.7
  144.3 4.7 %collective-permute-start.6 = (bf16[512,1,84]{0,2,1:T(8,128)(2,1)S(1)}, bf16[512,1,84]{0,2,1:T(8,128)(2,1)S(1)}, u32[]{:S(2)}, u32[]{:S(2)}) collective-permute-start(bf16[512,1,84]{0,2,1:T(8,128)(2,1)S(1)} %bitcast.226), channel_id=1, source_target_pairs={{0,8},{8,16},{16,24},{24,32},{32,40},{40,48},{48,56},{56,64},{64,7... | collective-permute-start | bytes 258056 | tf_op jit(solution)/shard_map/ppermute | solution.py:24
  149.1 1.5 collective-permute-done.6
  150.6 0.6 convolution_convert_fusion.1
  151.2 0.5 convolution_convert_fusion
  151.7 2.1 fusion.11
  153.8 2.2 fusion.31
  156.2 1.3 collective-permute-start.9
  157.5 4.7 %collective-permute-start.8 = (bf16[512,1,512]{0,2,1:T(8,128)(2,1)S(1)}, bf16[512,1,512]{0,2,1:T(8,128)(2,1)S(1)}, u32[]{:S(2)}, u32[]{:S(2)}) collective-permute-start(bf16[512,1,512]{0,2,1:T(8,128)(2,1)S(1)} %bitcast.222), channel_id=1, source_target_pairs={{0,8},{8,16},{16,24},{24,32},{32,40},{40,48},{48,56},{56,64},{64,7... | collective-permute-start | bytes 1572872 | tf_op jit(solution)/shard_map/ppermute | solution.py:24
  162.3 1.1 fusion.94
  163.4 1.4 fusion.99
  164.8 3.3 collective-permute-done.9
  168.1 0.9 collective-permute-done.8
  169.0 0.2 fusion.62
  169.2 2.5 fusion.69
  172.4 81.9 %psum.28 = f32[]{:T(128)} all-reduce(f32[]{:T(128)S(6)} %mul.282), channel_id=1, replica_groups=mesh['band'=16,'chan'=4,'member'=2] {'band','chan','member'}, use_global_device_ids=true, to_apply=%region_6.7 | all-reduce | flops 1 | bytes 8 | tf_op jit(solution)/shard_map/psum | solution.py:186
  255.0 84.8 %all-reduce.3.cloned.1.call-done = (f32[512,84]{0,1:T(8,128)}, f32[512,512]{1,0:T(8,128)}, f32[512,512]{1,0:T(8,128)}) async-done(((f32[512,84]{0,1:T(8,128)}, f32[512,512]{1,0:T(8,128)}, f32[512,512]{1,0:T(8,128)}), (f32[512,84]{0,1:T(8,128)}, f32[512,512]{1,0:T(8,128)}, f32[512,512]{1,0:T(8,128)})) %all-reduce.3.cloned.1.call-update) | async-done | bytes 2269200 | tf_op jit(solution)/shard_map/psum | solution.py:186
  339.8 1.7 copy.44
  341.5 2.3 copy.45
  343.7 1.0 copy.46
  (52 shorter events, 1.0 us)
Async XLA Ops:
  7.2 13.0 %copy-start = (bf16[512,512]{1,0:T(8,128)(2,1)S(1)}, bf16[512,512]{1,0:T(8,128)(2,1)}, u32[]{:S(2)}) copy-start(bf16[512,512]{1,0:T(8,128)(2,1)} %param.19) | copy-start | bytes 1572868
  7.2 332.6 %all-reduce.3.cloned.1.call-start = ((), (), s32[]{:S(2)}) async-start(), calls=%async_computation | async-start | bytes 4554752 | tf_op jit(solution)/shard_map/psum | solution.py:186
  16.1 2.8 copy-start.2
  23.2 1.7 copy-start.4
  24.8 6.5 %copy-start.15 = (f32[4]{0:T(128)S(1)}, f32[4]{0:T(128)}, u32[]{:S(2)}) copy-start(f32[4]{0:T(128)} %param.22) | copy-start | bytes 52
  24.8 6.6 %copy-start.10 = (s32[512,32]{0,1:T(8,128)S(1)}, s32[512,32]{0,1:T(8,128)}, u32[]{:S(2)}) copy-start(s32[512,32]{0,1:T(8,128)} %param.27) | copy-start | bytes 196612
  26.0 48.8 %collective-permute-start = (f32[512,1,512]{2,0,1:T(8,128)}, f32[512,1,512]{2,0,1:T(8,128)S(1)}, u32[]{:S(2)}, u32[]{:S(2)}) collective-permute-start(f32[512,1,512]{2,0,1:T(8,128)} %get-tuple-element.53), channel_id=1, source_target_pairs={{0,8},{8,16},{16,24},{24,32},{32,40},{40,48},{48,56},{56,64},{64,7... | collective-permute-start | bytes 3145736 | tf_op jit(solution)/shard_map/ppermute | solution.py:24
  30.1 44.7 %collective-permute-start.1 = (f32[512,1,512]{2,0,1:T(8,128)S(1)}, f32[512,1,512]{2,0,1:T(8,128)S(1)}, u32[]{:S(2)}, u32[]{:S(2)}) collective-permute-start(f32[512,1,512]{2,0,1:T(8,128)S(1)} %get-tuple-element.54), channel_id=1, source_target_pairs={{8,0},{16,8},{24,16},{32,24},{40,32},{48,40},{56,48},{64,56},{72,6... | collective-permute-start | bytes 3145736 | tf_op jit(solution)/shard_map/ppermute | solution.py:25
  31.5 44.7 %copy-start.12 = (f32[512]{0:T(512)S(1)}, f32[512]{0:T(512)}, u32[]{:S(2)}) copy-start(f32[512]{0:T(512)} %param.20) | copy-start | bytes 6148
  76.2 8.0 %copy-start.5 = (f32[512,1,512]{2,0,1:T(8,128)}, f32[512,1,512]{2,0,1:T(8,128)S(1)}, u32[]{:S(2)}) copy-start(f32[512,1,512]{2,0,1:T(8,128)S(1)} %get-tuple-element.48) | copy-start | bytes 3145732
  77.4 15.4 %collective-permute-start.3 = (bf16[512,1,512]{2,0,1:T(8,128)(2,1)}, bf16[512,1,512]{2,0,1:T(8,128)(2,1)}, u32[]{:S(2)}, u32[]{:S(2)}) collective-permute-start(bf16[512,1,512]{2,0,1:T(8,128)(2,1)} %multiply_convert_fusion.3), channel_id=1, source_target_pairs={{8,0},{16,8},{24,16},{32,24},{40,32},{48,40},{56,48},{64,56},{72,6... | collective-permute-start | bytes 1572872 | tf_op jit(solution)/shard_map/ppermute | solution.py:25
  78.7 15.0 %collective-permute-start.2 = (bf16[512,1,512]{2,0,1:T(8,128)(2,1)}, bf16[512,1,512]{2,0,1:T(8,128)(2,1)}, u32[]{:S(2)}, u32[]{:S(2)}) collective-permute-start(bf16[512,1,512]{2,0,1:T(8,128)(2,1)} %multiply_convert_fusion.3), channel_id=1, source_target_pairs={{0,8},{8,16},{16,24},{24,32},{32,40},{40,48},{48,56},{56,64},{64,7... | collective-permute-start | bytes 1572872 | tf_op jit(solution)/shard_map/ppermute | solution.py:24
  115.6 3.6 %copy-start.3 = (bf16[1,1536,1,512]{1,3,0,2:T(8,128)(2,1)S(1)}, bf16[1,1536,1,512]{1,3,0,2:T(8,128)(2,1)}, u32[]{:S(2)}) copy-start(bf16[1,1536,1,512]{1,3,0,2:T(8,128)(2,1)} %slice.134) | copy-start | bytes 4718596
  120.2 1.2 copy-start.6
  120.2 1.3 copy-start.7
  120.2 1.8 copy-start.9
  121.3 7.3 %copy-start.11 = (s32[2048]{0:T(1024)S(1)}, s32[2048]{0:T(1024)}, u32[]{:S(2)}) copy-start(s32[2048]{0:T(1024)} %param.26) | copy-start | bytes 24580
  122.3 7.0 %collective-permute-start.5 = (f32[512,1,84]{0,2,1:T(8,128)S(1)}, f32[512,1,84]{0,2,1:T(8,128)S(1)}, u32[]{:S(2)}, u32[]{:S(2)}) collective-permute-start(f32[512,1,84]{0,2,1:T(8,128)S(1)} %convolution_bitcast_fusion.2), channel_id=1, source_target_pairs={{8,0},{16,8},{24,16},{32,24},{40,32},{48,40},{56,48},{64,56},{72,6... | collective-permute-start | bytes 516104 | tf_op jit(solution)/shard_map/ppermute | solution.py:25
  123.6 7.2 %collective-permute-start.4 = (f32[512,1,84]{0,2,1:T(8,128)S(1)}, f32[512,1,84]{0,2,1:T(8,128)S(1)}, u32[]{:S(2)}, u32[]{:S(2)}) collective-permute-start(f32[512,1,84]{0,2,1:T(8,128)S(1)} %convolution_bitcast_fusion.2), channel_id=1, source_target_pairs={{0,8},{8,16},{16,24},{24,32},{32,40},{40,48},{48,56},{56,64},{64,7... | collective-permute-start | bytes 516104 | tf_op jit(solution)/shard_map/ppermute | solution.py:24
  133.9 3.0 copy-start.13
  133.9 3.0 copy-start.14
  133.9 3.0 copy-start.16
  143.0 6.1 %collective-permute-start.7 = (bf16[512,1,84]{0,2,1:T(8,128)(2,1)S(1)}, bf16[512,1,84]{0,2,1:T(8,128)(2,1)S(1)}, u32[]{:S(2)}, u32[]{:S(2)}) collective-permute-start(bf16[512,1,84]{0,2,1:T(8,128)(2,1)S(1)} %bitcast.227), channel_id=1, source_target_pairs={{8,0},{16,8},{24,16},{32,24},{40,32},{48,40},{56,48},{64,56},{72,6... | collective-permute-start | bytes 258056 | tf_op jit(solution)/shard_map/ppermute | solution.py:25
  144.3 6.3 %collective-permute-start.6 = (bf16[512,1,84]{0,2,1:T(8,128)(2,1)S(1)}, bf16[512,1,84]{0,2,1:T(8,128)(2,1)S(1)}, u32[]{:S(2)}, u32[]{:S(2)}) collective-permute-start(bf16[512,1,84]{0,2,1:T(8,128)(2,1)S(1)} %bitcast.226), channel_id=1, source_target_pairs={{0,8},{8,16},{16,24},{24,32},{32,40},{40,48},{48,56},{56,64},{64,7... | collective-permute-start | bytes 258056 | tf_op jit(solution)/shard_map/ppermute | solution.py:24
  156.2 11.9 %collective-permute-start.9 = (bf16[512,1,512]{0,2,1:T(8,128)(2,1)S(1)}, bf16[512,1,512]{0,2,1:T(8,128)(2,1)S(1)}, u32[]{:S(2)}, u32[]{:S(2)}) collective-permute-start(bf16[512,1,512]{0,2,1:T(8,128)(2,1)S(1)} %bitcast.224), channel_id=1, source_target_pairs={{8,0},{16,8},{24,16},{32,24},{40,32},{48,40},{56,48},{64,56},{72,6... | collective-permute-start | bytes 1572872 | tf_op jit(solution)/shard_map/ppermute | solution.py:25
  157.5 11.5 %collective-permute-start.8 = (bf16[512,1,512]{0,2,1:T(8,128)(2,1)S(1)}, bf16[512,1,512]{0,2,1:T(8,128)(2,1)S(1)}, u32[]{:S(2)}, u32[]{:S(2)}) collective-permute-start(bf16[512,1,512]{0,2,1:T(8,128)(2,1)S(1)} %bitcast.222), channel_id=1, source_target_pairs={{0,8},{8,16},{16,24},{24,32},{32,40},{40,48},{48,56},{56,64},{64,7... | collective-permute-start | bytes 1572872 | tf_op jit(solution)/shard_map/ppermute | solution.py:24
  171.7 173.0 %copy-start.1 = (bf16[512,512]{1,0:T(8,128)(2,1)S(1)}, bf16[512,512]{1,0:T(8,128)(2,1)}, u32[]{:S(2)}) copy-start(bf16[512,512]{1,0:T(8,128)(2,1)} %param.19) | copy-start | bytes 1572868
  339.8 4.0 %copy-start.8 = (f32[512,512]{1,0:T(8,128)S(1)}, f32[512,512]{1,0:T(8,128)}, u32[]{:S(2)}) copy-start(f32[512,512]{1,0:T(8,128)} %get-tuple-element.74) | copy-start | bytes 3145732
Sparse Core Ops, SparseCore 0:
  171.9 167.8 all-reduce.2
where the time goes:
time: 354 us; the launch traced here: 353 us
  waiting for transfers between devices  94.5 us (27%)
  blocking collectives  81.9 us (23%)
  other arithmetic  62.5 us (18%)
  matrix products  46.8 us (13%)
  starting transfers between devices  30.4 us (9%)
  local copies, waits for them, and re-layouts  18.9 us (5%)
  between operations  17.8 us (5%)
    psum x1, waiting for transfers between devices, local(): lax.psum((loss_part, grad_dec, grad_out, grad_value), ('band', 'chan', 'm...  84.8 us
    psum x1, blocking collectives, local(): lax.psum((loss_part, grad_dec, grad_out, grad_value), ('band', 'chan', 'm...  81.9 us
    reduce_sum x1, other arithmetic, block_weights(): jnp.sum((local_nbrs[:, :, None] == node_ids[None, None, :]).astype(jnp.fl...  43.2 us
    ppermute x5, starting transfers between devices, with_halo(): before = lax.ppermute(last, axis, up)  23.9 us
    dot_general x6, matrix products, split_einsum(): term = jnp.einsum(form, left, piece, preferred_element_type=jnp.float32)  12.3 us
    convert_element_type x8, other arithmetic, split_parts(): piece = lax.optimization_barrier(rest.astype(jnp.bfloat16))  9.76 us
    unnamed x37, local copies, waits for them, and re-layouts  7.56 us
    dot_general x1, matrix products, local(): jnp.einsum('gp,gmd->pmd', enc_table, hidden, preferred_element_type=jnp.f...  7.41 us
  transfers between devices with their start and end apart: 11, of which 8 were waited for; matrix products, arithmetic and copies ran while one was open for 15% of the time, Pallas kernels for 0%

commit v1 on v0

v1 whole, which is shorter than its diff:
```python
import math

import jax
import jax.numpy as jnp
from jax import lax
from jax.experimental import pallas as pl
from jax.experimental.pallas import tpu as pltpu
from jax.sharding import PartitionSpec as P

D = 512
VARS = 84
HEADS = 4
NBR = 32
G_DEV = 2048
M_DEV = 512
HEAD_DIM = 128
GRID = 32768
MEMBERS = 8
WINDOW = 3 * M_DEV
ROWS = 96
BF16, F32, I32 = jnp.bfloat16, jnp.float32, jnp.int32
MESH_ID = pl.DeviceIdType.MESH
SUM_ROWS = {"out": 2048, "value": 2048, "dec": 512}
SUM_AXES = {"out": ("x", "y", "z"), "value": ("y", "z", "x"), "dec": ("z", "x", "y")}


def coordinates():
    band, chan, core = (lax.axis_index("band"), lax.axis_index("chan"), lax.axis_index("member"))
    return {"band": band, "x": chan, "y": lax.rem(band, 4), "z": band // 4, "core": core}


def peer_on(axis, at, step):
    other = lax.rem(at[axis] + step, 4)
    if axis == "x":
        return (at["band"], other, at["core"])
    if axis == "y":
        return (at["z"] * 4 + other, at["x"], at["core"])
    return (other * 4 + at["y"], at["x"], at["core"])


def sibling(at):
    return (at["band"], at["x"], 1 - at["core"])


class Copies:
    def __init__(self, send_sems, recv_sems):
        self.send_sems, self.recv_sems, self.all = send_sems, recv_sems, []

    def start(self, source, target, device):
        used = len(self.all)
        copy = pltpu.make_async_remote_copy(
            src_ref=source,
            dst_ref=target,
            send_sem=self.send_sems.at[used],
            recv_sem=self.recv_sems.at[used],
            device_id=device,
            device_id_type=MESH_ID,
        )
        self.all.append(copy)
        copy.start()
        return copy


def greet(devices):
    barrier = pltpu.get_barrier_semaphore()
    for device in devices:
        pl.semaphore_signal(barrier, inc=1, device_id=device, device_id_type=MESH_ID)
    pl.semaphore_wait(barrier, len(devices))


def sum_partners(at):
    return [sibling(at)] + [peer_on(axis, at, step) for axis in ("x", "y", "z") for step in (1, 2, 3)]


def sum_scratch(rows):
    half = rows // 2
    return [
        pltpu.VMEM((rows, 128), F32),
        pltpu.VMEM((rows, 128), F32),
        pltpu.VMEM((half, 128), F32),
        pltpu.VMEM((half, 128), F32),
        pltpu.VMEM((3, half // 4, 128), F32),
        pltpu.VMEM((half // 4, 128), F32),
        pltpu.VMEM((3, half // 16, 128), F32),
        pltpu.VMEM((4, half // 16, 128), F32),
        pltpu.VMEM((half // 16, 128), F32),
    ]


def device_sum(name, refs, copies, at):
    part, total, near, pair, first_in, first, second_in, slots, second = refs
    first_axis, second_axis, third_axis = SUM_AXES[name]
    half = SUM_ROWS[name] // 2
    quarter, tiny = half // 4, half // 16

    def rows(start, size):
        return pl.ds(pl.multiple_of(start, size), size)

    def scatter(source, landing, size, axis):
        sent = []
        for step in (1, 2, 3):
            block = source.at[rows(lax.rem(at[axis] + step, 4) * size, size), :]
            sent.append(copies.start(block, landing.at[step - 1], peer_on(axis, at, step)))
        return sent

    def gather_sum(source, landing, size, axis, sent):
        for flight in sent:
            flight.wait_recv()
        return (source[rows(at[axis] * size, size), :] + landing[0]) + (landing[1] + landing[2])

    def spread(start, size, axis):
        block = total.at[rows(start, size), :]
        return [copies.start(block, block, peer_on(axis, at, step)) for step in (1, 2, 3)]

    mine = at["core"] * half
    flight = copies.start(part.at[rows((1 - at["core"]) * half, half), :], near, sibling(at))
    yield
    flight.wait_recv()
    pair[...] = part[rows(mine, half), :] + near[...]
    flights = scatter(pair, first_in, quarter, first_axis)
    yield
    first[...] = gather_sum(pair, first_in, quarter, first_axis, flights)
    flights = scatter(first, second_in, tiny, second_axis)
    yield
    second[...] = gather_sum(first, second_in, tiny, second_axis, flights)
    slots[at[third_axis]] = second[...]
    flights = [
        copies.start(second, slots.at[at[third_axis]], peer_on(third_axis, at, step)) for step in (1, 2, 3)
    ]
    yield
    for flight in flights:
        flight.wait_recv()
    outer = mine + at[first_axis] * quarter
    inner = outer + at[second_axis] * tiny
    total[rows(inner, tiny), :] = (slots[0] + slots[1]) + (slots[2] + slots[3])
    flights = spread(inner, tiny, second_axis)
    yield
    for flight in flights:
        flight.wait_recv()
    flights = spread(outer, quarter, first_axis)
    yield
    for flight in flights:
        flight.wait_recv()
    block = total.at[rows(mine, half), :]
    flight = copies.start(block, block, sibling(at))
    yield
    flight.wait_recv()
    yield


def dot(left, right):
    return jnp.dot(left, right, preferred_element_type=F32)


def dot_t(left, right):
    return lax.dot_general(left, right, (((1,), (1,)), ((), ())), preferred_element_type=F32)


def pieces_of(values, count):
    pieces, rest = ([], values)
    for index in range(count):
        piece = rest.astype(BF16)
        pieces.append(piece)
        if index + 1 < count:
            rest = rest - piece.astype(F32)
    return pieces


def column_of(row, size):
    tall = jnp.transpose(jnp.broadcast_to(row, (128, size)))
    return tall


def unit_heads(values, width):
    split = values.reshape(HEADS, HEAD_DIM, width)
    scale = lax.rsqrt(jnp.mean(split * split, axis=1, keepdims=True) + 1e-06)
    return (split * scale).reshape(D, width)


def lanes(values, width):
    return jnp.concatenate([values] * (width // 128), axis=1)


def step_kernel(
    noisy_ref,
    target_ref,
    level_ref,
    var_ref,
    embed_in_ref,
    embed_out_ref,
    gain_ref,
    qkv_ref,
    head_scale_ref,
    out_w_ref,
    dec_w_ref,
    g2m_ref,
    m2g_ref,
    nbr_ref,
    lat_ref,
    out_result,
    value_result,
    dec_result,
    *scratch,
):
    send_sems, recv_sems = scratch[:2]
    (
        state_in,
        g2m_in,
        pad_in,
        pad_dec,
        embed_in_t,
        embed_out_t,
        q_t,
        k_t,
        v_t,
        out_t,
        dec_t,
        node_hidden,
        mesh_in,
        normed,
        normed_in,
        unit_q,
        unit_k,
        values,
        counts,
        counts_16,
        exps,
        probs,
        attended,
        mesh_out,
        table,
        vars_own,
        vars_16,
        vars_in,
        net,
        grad_net,
        node_out,
        node_in,
        node_own,
        mesh_grad,
        head_grad,
        value_out,
        value_in,
        value_own,
    ) = scratch[2:40]
    sums = {name: scratch[40 + 9 * i : 49 + 9 * i] for i, name in enumerate(("out", "value", "dec"))}
    at = coordinates()
    band = at["band"]
    left = (lax.rem(band + 15, 16), at["x"], at["core"])
    right = (lax.rem(band + 1, 16), at["x"], at["core"])
    sides = ((0, left, 1), (1, right, 0))
    base = band * M_DEV
    copies = Copies(send_sems, recv_sems)

    greet([left, right] + sum_partners(at))

    state_flights, node_flights = ([], [])
    for side, device, slot in sides:
        node_flights.append(copies.start(g2m_ref, g2m_in.at[slot], device))
    for chunk in range(4):
        cells = pl.ds(512 * chunk, 512)
        state_flights.append(
            [
                copies.start(noisy_ref.at[0, :, cells], state_in.at[slot, :, cells], device)
                for side, device, slot in sides
            ]
        )

    pad_in[...] = jnp.zeros_like(pad_in)
    pad_dec[...] = jnp.zeros_like(pad_dec)
    pad_in[:VARS, :] = embed_in_ref[...]
    pad_dec[:, :VARS] = dec_w_ref[...]
    embed_in_t[...] = jnp.transpose(pad_in[...])
    dec_t[...] = jnp.transpose(pad_dec[...])
    embed_out_t[...] = jnp.transpose(embed_out_ref[...])
    q_t[...] = jnp.transpose(qkv_ref[0])
    k_t[...] = jnp.transpose(qkv_ref[1])
    v_t[...] = jnp.transpose(qkv_ref[2])
    out_t[...] = jnp.transpose(out_w_ref[...])

    level = jnp.full((1, 1), level_ref[0], F32)
    level_sq = level * level + 1.0
    scale_in = lax.rsqrt(level_sq)
    skip_scale = 1.0 / level_sq
    out_scale = level * scale_in
    half_scale = 0.5 * scale_in

    def encode(state, nodes):
        half_t = dot(embed_in_t[:, :VARS], state) * half_scale
        hidden = (half_t + half_t * jnp.tanh(half_t)).astype(BF16)
        ids = lax.broadcasted_iota(I32, (M_DEV, 512), 0)
        chosen = jnp.where(nodes - base == ids, 1.0, 0.0).astype(BF16)
        node_hidden[...] += dot_t(hidden, chosen)

    node_hidden[...] = jnp.zeros_like(node_hidden)

    @pl.loop(0, 4)
    def _(chunk):
        cells = pl.ds(pl.multiple_of(chunk * 512, 512), 512)
        encode(noisy_ref[0, :, cells], g2m_ref[:, cells])

    @pl.loop(0, 8)
    def _(block):
        ids = lax.broadcasted_iota(I32, (64, M_DEV), 0) + block * 64
        total = jnp.zeros((64, M_DEV), I32)
        for j in range(NBR):
            near = nbr_ref[j : j + 1, :] - (base - M_DEV)
            patch = near // M_DEV
            within = near - patch * M_DEV
            field = jnp.where(patch == 0, 64, jnp.where(patch == 1, 1, 4096))
            total = total + jnp.where(within == ids, field, 0)
        chunk = block // 2
        part = (block - 2 * chunk) * 64
        for start, shift in (
            (block * 64, 0),
            (M_DEV + 256 * chunk + part, 6),
            (M_DEV + 256 * chunk + 128 + part, 12),
        ):
            count = lax.shift_right_logical(total, jnp.full_like(total, shift)) & 63
            rows = pl.ds(pl.multiple_of(start, 64), 64)
            counts[rows, :] = count.astype(F32)
            counts_16[rows, :] = count.astype(F32).astype(BF16)

    for block in range(12):
        if block < 4:
            offset = 128 * block
        else:
            offset = 128 * ((block - 4) // 2) + (M_DEV if (block - 4) % 2 else -M_DEV)
        ids = lax.broadcasted_iota(I32, (128, G_DEV), 0) + (base + offset)
        table[128 * block : 128 * block + 128, :] = jnp.where(m2g_ref[...] == ids, 1.0, 0.0).astype(BF16)

    for flight in node_flights:
        flight.wait_recv()
    for chunk in range(4):
        cells = slice(512 * chunk, 512 * chunk + 512)
        for flight in state_flights[chunk]:
            flight.wait_recv()

        @pl.loop(0, 2)
        def _(slot):
            encode(state_in[slot, :, cells], g2m_in[slot, :, cells])

    encoded = None
    for piece in pieces_of(node_hidden[...], 3):
        term = dot(embed_out_t[...], piece)
        encoded = term if encoded is None else encoded + term
    mesh_in[...] = encoded
    mean_sq = jnp.mean(encoded * encoded, axis=0, keepdims=True)
    gain = lanes(column_of(gain_ref[...], D), M_DEV)
    normed[...] = (encoded * lax.rsqrt(mean_sq + 1e-05) * gain).astype(BF16)

    normed_flights = []
    for chunk in range(4):
        normed_flights.append(
            [
                copies.start(
                    normed.at[:, pl.ds(128 * chunk, 128)],
                    normed_in.at[:, pl.ds(256 * chunk + 128 * slot, 128)],
                    device,
                )
                for side, device, slot in sides
            ]
        )

    unit_q[...] = unit_heads(dot(q_t[...], normed[...]), M_DEV).astype(BF16)

    def attend(near, start, width):
        keys = unit_heads(dot(k_t[...], near), width).astype(BF16)
        unit_k[start : start + width, :] = jnp.transpose(keys)
        values[:, start : start + width] = dot(v_t[...], near).astype(BF16)
        sums_now = []
        count = counts[start : start + width, :]
        for head in range(HEADS):
            part = slice(HEAD_DIM * head, HEAD_DIM * head + HEAD_DIM)
            scores = dot(unit_k[start : start + width, part], unit_q[part, :])
            exp = jnp.exp(scores * (head_scale_ref[head] / HEAD_DIM))
            exps[head, start : start + width, :] = exp
            sums_now.append(jnp.sum(exp * count, axis=0, keepdims=True))
        return sums_now

    exp_sums = None
    for chunk in range(6):
        if chunk < 2:
            near = normed[:, 256 * chunk : 256 * chunk + 256]
        else:
            for flight in normed_flights[chunk - 2]:
                flight.wait_recv()
            near = normed_in[:, 256 * (chunk - 2) : 256 * (chunk - 2) + 256]
        sums_now = attend(near, 256 * chunk, 256)
        exp_sums = sums_now if exp_sums is None else [a + b for a, b in zip(exp_sums, sums_now)]

    for head in range(HEADS):
        inverse = 1.0 / exp_sums[head]
        part = slice(HEAD_DIM * head, HEAD_DIM * head + HEAD_DIM)

        @pl.loop(0, 6)
        def _(block):
            rows = pl.ds(pl.multiple_of(block * 256, 256), 256)
            prob = (exps[head, rows, :] * inverse).astype(BF16)
            probs[head, rows, :] = prob * counts_16[rows, :]

        attended[part, :] = dot(values[part, :], probs[head]).astype(BF16)

    mesh_out[...] = (mesh_in[...] + dot(out_t[...], attended[...])).astype(BF16)
    vars_own[...] = dot(dec_t[:ROWS, :], mesh_out[...])

    vars_flights = []
    for chunk in range(4):
        vars_flights.append(
            [
                copies.start(
                    vars_own.at[:, pl.ds(128 * chunk, 128)],
                    vars_in.at[:, pl.ds(256 * chunk + 128 * slot, 128)],
                    device,
                )
                for side, device, slot in sides
            ]
        )

    def split_rows(source):
        for index, piece in enumerate(pieces_of(source, 2)):
            vars_16[ROWS * index : ROWS * index + ROWS, : source.shape[1]] = piece

    def decode(width, start, first):
        @pl.loop(0, 4)
        def _(chunk):
            cells = pl.ds(pl.multiple_of(chunk * 512, 512), 512)
            both = dot(vars_16[:, :width], table[start : start + width, cells])
            term = both[:ROWS, :] + both[ROWS:, :]
            net[:, cells] = term if first else net[:, cells] + term

    split_rows(vars_own[...])
    decode(M_DEV, 0, True)
    for pair in vars_flights:
        for flight in pair:
            flight.wait_recv()
    split_rows(vars_in[...])
    decode(2 * M_DEV, M_DEV, False)

    square = lax.broadcasted_iota(I32, (VARS, VARS), 0) == lax.broadcasted_iota(I32, (VARS, VARS), 1)
    var_column = jnp.sum(jnp.where(square, var_ref[...], 0.0), axis=1, keepdims=True)
    weights = var_column * lat_ref[...]
    errors = (
        skip_scale * noisy_ref[0].astype(F32) + out_scale * net[:VARS, :] - target_ref[0].astype(F32)
    )
    scale_all = 1.0 / (MEMBERS * VARS)
    loss = jnp.sum(jnp.sum(weights * errors * errors, axis=1, keepdims=True), axis=0, keepdims=True) * scale_all
    grad_net[...] = jnp.zeros_like(grad_net)
    grad_net[:VARS, :] = ((2.0 * out_scale * scale_all) * weights * errors).astype(BF16)

    node_part = dot_t(grad_net[...], table[M_DEV:, :])
    for chunk in range(4):
        for side in (0, 1):
            start = 256 * chunk + 128 * side
            node_out[side, :, 128 * chunk : 128 * chunk + 128] = node_part[:, start : start + 128].astype(BF16)
    node_flights = [
        copies.start(node_out.at[side], node_in.at[slot], device) for side, device, slot in sides
    ]
    node_own[...] = dot_t(grad_net[...], table[:M_DEV, :])
    for flight in node_flights:
        flight.wait_recv()
    node_grad = node_own[...] + node_in[0].astype(F32) + node_in[1].astype(F32)
    node_pieces = pieces_of(node_grad, 3)
    grown = None
    for piece in node_pieces:
        term = dot(dec_w_ref[...], piece[:VARS, :])
        grown = term if grown is None else grown + term
    mesh_grad[...] = grown.astype(BF16)
    head_grad[...] = dot(out_w_ref[...], mesh_grad[...]).astype(BF16)

    value_flights = []
    for head in range(HEADS):
        part = slice(HEAD_DIM * head, HEAD_DIM * head + HEAD_DIM)
        spread = dot_t(head_grad[part, :], probs[head, M_DEV:, :])
        for chunk in range(4):
            for side in (0, 1):
                start = 256 * chunk + 128 * side
                value_out[side, part, 128 * chunk : 128 * chunk + 128] = spread[
                    :, start : start + 128
                ].astype(BF16)
        rows = pl.ds(HEAD_DIM * head, HEAD_DIM)
        value_flights.append(
            [
                copies.start(value_out.at[side, rows, :], value_in.at[slot, rows, :], device)
                for side, device, slot in sides
            ]
        )

    def store_square(target, source):
        for lane in range(4):
            target[512 * lane : 512 * lane + 512, :] = source[:, 128 * lane : 128 * lane + 128]

    store_square(sums["out"][0], dot_t(attended[...], mesh_grad[...]))
    dec_sum = None
    for piece in node_pieces:
        term = dot_t(mesh_out[...], piece)
        dec_sum = term if dec_sum is None else dec_sum + term
    sums["dec"][0][...] = jnp.zeros_like(sums["dec"][0])
    sums["dec"][0][:, :ROWS] = dec_sum
    corner = (lax.broadcasted_iota(I32, (8, 128), 0) == 0) & (lax.broadcasted_iota(I32, (8, 128), 1) == 127)
    sums["dec"][0][:8, :] = jnp.where(corner, loss, sums["dec"][0][:8, :])
    out_sum = device_sum("out", sums["out"], copies, at)
    dec_sum = device_sum("dec", sums["dec"], copies, at)
    next(out_sum)
    next(dec_sum)
    for head in range(HEADS):
        part = slice(HEAD_DIM * head, HEAD_DIM * head + HEAD_DIM)
        value_own[part, :] = dot_t(head_grad[part, :], probs[head, :M_DEV, :])
    next(out_sum)
    next(dec_sum)
    for head in range(HEADS):
        part = slice(HEAD_DIM * head, HEAD_DIM * head + HEAD_DIM)
        for flight in value_flights[head]:
            flight.wait_recv()
        grad = value_own[part, :] + value_in[0, part, :].astype(F32) + value_in[1, part, :].astype(F32)
        sums["value"][0][512 * head : 512 * head + 512, :] = dot_t(normed[...], grad.astype(BF16))
    value_sum = device_sum("value", sums["value"], copies, at)
    next(value_sum)
    for stage in range(6):
        next(value_sum)
        if stage < 5:
            next(out_sum)
            next(dec_sum)
        if stage == 5:
            next(value_sum)
    next(out_sum)
    next(dec_sum)
    for lane in range(4):
        for name, result in (("out", out_result), ("value", value_result)):
            result[:, 128 * lane : 128 * lane + 128] = sums[name][1][512 * lane : 512 * lane + 512, :]
    dec_result[...] = sums["dec"][1][...]
    for copy in copies.all:
        copy.wait_send()


def local(
    noisy_state,
    target_state,
    noise_level,
    var_weight,
    embed_in,
    embed_out,
    norm_gain,
    qkv_weight,
    head_scale,
    out_weight,
    dec_weight,
    g2m_node,
    m2g_node,
    neighbours,
):
    band = lax.axis_index("band")
    positions = (band * G_DEV + jnp.arange(G_DEV)).astype(F32)
    lat_weight = 0.2 + jnp.cos(math.pi * (positions + 0.5) / GRID - 0.5 * math.pi)
    vmem = pl.BlockSpec(memory_space=pltpu.VMEM)
    smem = pl.BlockSpec(memory_space=pltpu.SMEM)
    square = jax.ShapeDtypeStruct((D, D), F32)
    scratch = [
        pltpu.SemaphoreType.DMA((96,)),
        pltpu.SemaphoreType.DMA((96,)),
        pltpu.VMEM((2, VARS, G_DEV), BF16),
        pltpu.VMEM((2, 1, G_DEV), I32),
        pltpu.VMEM((128, D), BF16),
        pltpu.VMEM((D, 128), BF16),
        pltpu.VMEM((D, 128), BF16),
        pltpu.VMEM((D, D), BF16),
        pltpu.VMEM((D, D), BF16),
        pltpu.VMEM((D, D), BF16),
        pltpu.VMEM((D, D), BF16),
        pltpu.VMEM((D, D), BF16),
        pltpu.VMEM((128, D), BF16),
        pltpu.VMEM((D, M_DEV), F32),
        pltpu.VMEM((D, M_DEV), F32),
        pltpu.VMEM((D, M_DEV), BF16),
        pltpu.VMEM((D, 2 * M_DEV), BF16),
        pltpu.VMEM((D, M_DEV), BF16),
        pltpu.VMEM((WINDOW, D), BF16),
        pltpu.VMEM((D, WINDOW), BF16),
        pltpu.VMEM((WINDOW, M_DEV), F32),
        pltpu.VMEM((WINDOW, M_DEV), BF16),
        pltpu.VMEM((HEADS, WINDOW, M_DEV), F32),
        pltpu.VMEM((HEADS, WINDOW, M_DEV), BF16),
        pltpu.VMEM((D, M_DEV), BF16),
        pltpu.VMEM((D, M_DEV), BF16),
        pltpu.VMEM((WINDOW, G_DEV), BF16),
        pltpu.VMEM((ROWS, M_DEV), F32),
        pltpu.VMEM((2 * ROWS, 2 * M_DEV), BF16),
        pltpu.VMEM((ROWS, 2 * M_DEV), F32),
        pltpu.VMEM((ROWS, G_DEV), F32),
        pltpu.VMEM((ROWS, G_DEV), BF16),
        pltpu.VMEM((2, ROWS, M_DEV), BF16),
        pltpu.VMEM((2, ROWS, M_DEV), BF16),
        pltpu.VMEM((ROWS, M_DEV), F32),
        pltpu.VMEM((D, M_DEV), BF16),
        pltpu.VMEM((D, M_DEV), BF16),
        pltpu.VMEM((2, D, M_DEV), BF16),
        pltpu.VMEM((2, D, M_DEV), BF16),
        pltpu.VMEM((D, M_DEV), F32),
    ]
    for name in ("out", "value", "dec"):
        scratch += sum_scratch(SUM_ROWS[name])
    grad_out, grad_value, dec = pl.pallas_call(
        step_kernel,
        out_shape=(square, square, jax.ShapeDtypeStruct((D, 128), F32)),
        in_specs=[vmem, vmem, smem, vmem, vmem, vmem, vmem, vmem, smem] + [vmem] * 6,
        out_specs=(vmem,) * 3,
        scratch_shapes=scratch,
        compiler_params=pltpu.CompilerParams(
            collective_id=0, has_side_effects=True, vmem_limit_bytes=67043328
        ),
        name="step",
    )(
        noisy_state,
        target_state,
        noise_level,
        var_weight.reshape(1, VARS),
        embed_in,
        embed_out,
        norm_gain.reshape(1, D),
        qkv_weight,
        head_scale,
        out_weight,
        dec_weight,
        g2m_node.reshape(1, G_DEV),
        m2g_node.reshape(1, G_DEV),
        neighbours.T,
        lat_weight.reshape(1, G_DEV),
    )
    return dec[0, 127] / GRID, dec[:, :VARS], grad_out, grad_value


def solution(mesh):
    in_specs = (
        P(("chan", "member"), None, "band"),
        P(("chan", "member"), None, "band"),
        P(("chan", "member")),
        P(),
        P(),
        P(),
        P(),
        P(),
        P(),
        P(),
        P(),
        P("band"),
        P("band"),
        P("band", None),
    )
    out_specs = (P(), P(), P(), P())
    return jax.shard_map(local, mesh=mesh, in_specs=in_specs, out_specs=out_specs, check_vma=False)
```

time: 354 us -> 122 us (0.34)
  Pallas kernels: 0 us -> 109 us
  waiting for transfers between devices: 94.5 us -> 0 us
  blocking collectives: 81.9 us -> 0 us
  other arithmetic: 62.5 us -> 0.84 us
  matrix products: 46.8 us -> 0 us
  starting transfers between devices: 30.4 us -> 0 us
  between operations: 17.8 us -> 3.08 us
  local copies, waits for them, and re-layouts: 18.9 us -> 8.01 us
    pallas_call x0 -> x1, Pallas kernels: none -> 109 us  [local(): pl.pallas_call(step_kernel, out_shape=(square, square, jax.ShapeDtypeStru...]
    psum x1 -> x0, waiting for transfers between devices: 84.8 us -> none  [local(): lax.psum((loss_part, grad_dec, grad_out, grad_value), ('band', 'chan', 'm...]
    psum x1 -> x0, blocking collectives: 81.9 us -> none  [local(): lax.psum((loss_part, grad_dec, grad_out, grad_value), ('band', 'chan', 'm...]
    dot_general x22 -> x0, matrix products: 46.8 us -> none  [the longest x6 12.3 us: split_einsum(): term = jnp.einsum(form, left, piece, preferred_element_type=jnp.float32)]
    reduce_sum x3 -> x0, other arithmetic: 46.8 us -> none  [the longest x1 43.2 us: block_weights(): jnp.sum((local_nbrs[:, :, None] == node_ids[None, None, :]).astype(jnp.fl...]
    ppermute x10 -> x0, starting transfers between devices: 30.3 us -> none  [the longest x5 23.9 us: with_halo(): before = lax.ppermute(last, axis, up)]
    convert_element_type x10 -> x0, other arithmetic: 11.2 us -> none  [the longest x8 9.76 us: split_parts(): piece = lax.optimization_barrier(rest.astype(jnp.bfloat16))]
    ppermute x10 -> x0, waiting for transfers between devices: 9.64 us -> none  [the longest x5 4.84 us: with_halo(): after = lax.ppermute(leading, axis, down)]
  transfers between devices with their start and end apart: 11 -> 0, of which waited for: 8 -> 0; matrix products, arithmetic and copies ran while one was open for 15% -> 0% of each run, Pallas kernels for 0% -> 0%
where the time goes in v1:
time: 122 us; the launch traced here: 121 us
  Pallas kernels  109 us (89%)
  local copies, waits for them, and re-layouts  8.01 us (7%)
  between operations  3.08 us (3%)
    pallas_call x1, Pallas kernels, local(): pl.pallas_call(step_kernel, out_shape=(square, square, jax.ShapeDtypeStru...  109 us
    unnamed x6, local copies, waits for them, and re-layouts  6.75 us

profile of v1, /device:TPU:1, one launch (start us, length us, event | category | flops | bytes accessed | tf_op | source)
XLA Modules:
  0.0 121.2 jit_solution(16415263720026339709)
XLA Ops:
  0.6 1.7 %copy.18.dec_w_ref = bf16[512,84]{1,0:T(8,128)(2,1)} copy(bf16[512,84]{0,1:T(8,128)(2,1)} %param.24) | data formatting | bytes 172032 | tf_op args[10]
  2.3 0.8 cosine_add_fusion.lat_ref
  3.8 109.3 %step.1 = (f32[512,512]{1,0:T(8,128)}, f32[512,512]{1,0:T(8,128)}, f32[512,128]{1,0:T(8,128)}) custom-call(bf16[1,84,2048]{2,1,0:T(8,128)(2,1)} %noisy_ref.1, bf16[1,84,2048]{2,1,0:T(8,128)(2,1)} %target_ref.1, f32[1]{0:T(128)S(6)} %copy.22.level_ref, f32[1,84]{1,0:T(1,128)} %bitcast.12, bf16[84,512]{1,0:T(8,128)(2,1)} %embed_in_ref.1, ...), custom_call_target="tpu_custom_call" | custom-call | tf_op jit(solution)/shard_map/step/pallas_call | solution.py:602
  113.1 0.0 copy-start
  113.1 1.8 %copy.19 = f32[512,84]{0,1:T(8,128)} copy(f32[512,84]{1,0:T(8,128)} %bitcast.7) | data formatting | bytes 344064
  115.0 1.3 %slice.6 = f32[1,1]{1,0:T(1,128)} slice(f32[512,128]{1,0:T(8,128)} %get-tuple-element.7), slice={[0:1], [127:128]} | slice | bytes 8 | tf_op jit(solution)/shard_map/slice | solution.py:629
  116.9 2.3 %copy.23 = f32[512,512]{1,0:T(8,128)} copy(f32[512,512]{1,0:T(8,128)} %get-tuple-element.20) | data formatting | bytes 2097152
  119.1 0.0 copy-done
  119.1 1.0 copy.24
Async XLA Ops:
  113.1 6.0 %copy-start = (f32[512,512]{1,0:T(8,128)S(1)}, f32[512,512]{1,0:T(8,128)}, u32[]{:S(2)}) copy-start(f32[512,512]{1,0:T(8,128)} %get-tuple-element.21) | copy-start | bytes 3145732

commit v2 on v1

v2 whole, which is shorter than its diff:
```python
import math

import jax
import jax.numpy as jnp
from jax import lax
from jax.experimental import pallas as pl
from jax.experimental.pallas import tpu as pltpu
from jax.sharding import PartitionSpec as P

D = 512
VARS = 84
HEADS = 4
NBR = 32
G_DEV = 2048
M_DEV = 512
HEAD_DIM = 128
GRID = 32768
MEMBERS = 8
WINDOW = 3 * M_DEV
ROWS = 96
BF16, F32, I32 = jnp.bfloat16, jnp.float32, jnp.int32
MESH_ID = pl.DeviceIdType.MESH
UNITS = (
    ("out", 0, 1024, ("x", "z", "y")),
    ("out", 1024, 1024, ("x", "y", "z")),
    ("dec", 0, 512, ("x", "z", "y")),
    ("value", 0, 512, ("z", "y", "x")),
    ("value", 512, 512, ("y", "z", "x")),
    ("value", 1024, 512, ("z", "y", "x")),
    ("value", 1536, 512, ("y", "z", "x")),
)


def coordinates():
    band, chan, core = (lax.axis_index("band"), lax.axis_index("chan"), lax.axis_index("member"))
    return {"band": band, "x": chan, "y": lax.rem(band, 4), "z": band // 4, "core": core}


def peer_on(axis, at, step):
    other = lax.rem(at[axis] + step, 4)
    if axis == "x":
        return (at["band"], other, at["core"])
    if axis == "y":
        return (at["z"] * 4 + other, at["x"], at["core"])
    return (other * 4 + at["y"], at["x"], at["core"])


def sibling(at):
    return (at["band"], at["x"], 1 - at["core"])


class Flight:
    def __init__(self, copies, index, size_ref, device):
        self.whole = pltpu.make_async_remote_copy(
            src_ref=size_ref,
            dst_ref=size_ref,
            send_sem=copies.send_sems.at[index],
            recv_sem=copies.recv_sems.at[index],
            device_id=device,
            device_id_type=MESH_ID,
        )

    def wait_recv(self):
        self.whole.wait_recv()

    def wait_send(self):
        self.whole.wait_send()


class Copies:
    def __init__(self, send_sems, recv_sems):
        self.send_sems, self.recv_sems, self.all = send_sems, recv_sems, []

    def start(self, size_ref, group):
        index = len(self.all)
        for source, target, device in group:
            pltpu.make_async_remote_copy(
                src_ref=source,
                dst_ref=target,
                send_sem=self.send_sems.at[index],
                recv_sem=self.recv_sems.at[index],
                device_id=device,
                device_id_type=MESH_ID,
            ).start()
        self.all.append(Flight(self, index, size_ref, group[0][2]))
        return self.all[-1]


def greet(devices):
    for device in devices:
        pl.semaphore_signal(
            pltpu.get_barrier_semaphore(), inc=1, device_id=device, device_id_type=MESH_ID
        )


def await_greetings(devices):
    pl.semaphore_wait(pltpu.get_barrier_semaphore(), len(devices))


def sum_partners(at):
    return [sibling(at)] + [peer_on(axis, at, step) for axis in ("x", "y", "z") for step in (1, 2, 3)]


def sum_scratch(rows):
    half = rows // 2
    return [
        pltpu.VMEM((half, 128), F32),
        pltpu.VMEM((half, 128), F32),
        pltpu.VMEM((3, half // 4, 128), F32),
        pltpu.VMEM((half // 4, 128), F32),
        pltpu.VMEM((3, half // 16, 128), F32),
        pltpu.VMEM((4, half // 16, 128), F32),
        pltpu.VMEM((half // 16, 128), F32),
    ]


def device_sum(part, total, unit, refs, copies, at):
    near, pair, first_in, first, second_in, slots, second = refs
    origin, size_all, (first_axis, second_axis, third_axis) = unit[1:]
    half = size_all // 2
    quarter, tiny = half // 4, half // 16

    def rows(start, size):
        return pl.ds(pl.multiple_of(start, size), size)

    def scatter(source, landing, size, axis):
        group = []
        for step in (1, 2, 3):
            block = source.at[rows(lax.rem(at[axis] + step, 4) * size, size), :]
            group.append((block, landing.at[step - 1], peer_on(axis, at, step)))
        return copies.start(landing, group)

    def gather_sum(source, landing, size, axis, flight):
        flight.wait_recv()
        return (source[rows(at[axis] * size, size), :] + landing[0]) + (landing[1] + landing[2])

    def spread(start, size, axis):
        block = total.at[rows(start, size), :]
        return copies.start(
            total.at[rows(0, 3 * size), :], [(block, block, peer_on(axis, at, step)) for step in (1, 2, 3)]
        )

    mine = origin + at["core"] * half
    flight = copies.start(
        near, [(part.at[rows(origin + (1 - at["core"]) * half, half), :], near, sibling(at))]
    )
    yield
    flight.wait_recv()
    pair[...] = part[rows(mine, half), :] + near[...]
    flight = scatter(pair, first_in, quarter, first_axis)
    yield
    first[...] = gather_sum(pair, first_in, quarter, first_axis, flight)
    flight = scatter(first, second_in, tiny, second_axis)
    yield
    second[...] = gather_sum(first, second_in, tiny, second_axis, flight)
    slots[at[third_axis]] = second[...]
    flight = copies.start(
        slots.at[pl.ds(0, 3)],
        [(second, slots.at[at[third_axis]], peer_on(third_axis, at, step)) for step in (1, 2, 3)],
    )
    yield
    flight.wait_recv()
    outer = mine + at[first_axis] * quarter
    inner = outer + at[second_axis] * tiny
    total[rows(inner, tiny), :] = (slots[0] + slots[1]) + (slots[2] + slots[3])
    flight = spread(inner, tiny, second_axis)
    yield
    flight.wait_recv()
    flight = spread(outer, quarter, first_axis)
    yield
    flight.wait_recv()
    block = total.at[rows(mine, half), :]
    flight = copies.start(block, [(block, block, sibling(at))])
    yield
    flight.wait_recv()
    yield


def dot(left, right):
    return jnp.dot(left, right, preferred_element_type=F32)


def dot_t(left, right):
    return lax.dot_general(left, right, (((1,), (1,)), ((), ())), preferred_element_type=F32)


def pieces_of(values, count):
    pieces, rest = ([], values)
    for index in range(count):
        piece = rest.astype(BF16)
        pieces.append(piece)
        if index + 1 < count:
            rest = rest - piece.astype(F32)
    return pieces


def column_of(row, size):
    tall = jnp.transpose(jnp.broadcast_to(row, (128, size)))
    return tall


def unit_heads(values, width):
    split = values.reshape(HEADS, HEAD_DIM, width)
    scale = lax.rsqrt(jnp.mean(split * split, axis=1, keepdims=True) + 1e-06)
    return (split * scale).reshape(D, width)


def lanes(values, width):
    return jnp.concatenate([values] * (width // 128), axis=1)


class Phase:
    def __init__(self):
        self.scope = None

    def __call__(self, name):
        if self.scope is not None:
            self.scope.__exit__(None, None, None)
        self.scope = None if name is None else jax.named_scope(name)
        if self.scope is not None:
            self.scope.__enter__()


STEP_VMEM = 57 << 20
INPUTS = (
    ("noisy", (VARS, G_DEV), BF16),
    ("g2m", (1, G_DEV), I32),
    ("embed_in", (VARS, D), BF16),
    ("embed_out", (D, D), BF16),
    ("gain", (1, D), F32),
    ("qkv", (3, D, D), BF16),
    ("nbr", (NBR, M_DEV), I32),
    ("m2g", (1, G_DEV), I32),
    ("out_w", (D, D), BF16),
    ("dec_w", (VARS, D), BF16),
    ("target", (VARS, G_DEV), BF16),
    ("var", (1, VARS), F32),
)

SCRATCH = (
    ("state_in", (2, VARS, G_DEV), BF16),
    ("g2m_in", (2, 1, G_DEV), I32),
    ("pad_in", (128, D), BF16),
    ("embed_in_t", (D, 128), BF16),
    ("dec_t", (128, D), BF16),
    ("dec_full", (D, 128), BF16),
    ("embed_out_t", (D, D), BF16),
    ("q_t", (D, D), BF16),
    ("k_t", (D, D), BF16),
    ("v_t", (D, D), BF16),
    ("out_t", (D, D), BF16),
    ("node_hidden", (D, M_DEV), F32),
    ("mesh_in", (D, M_DEV), F32),
    ("normed", (D, M_DEV), BF16),
    ("normed_in", (D, 2 * M_DEV), BF16),
    ("unit_q", (D, M_DEV), BF16),
    ("unit_k", (WINDOW, D), BF16),
    ("values", (D, WINDOW), BF16),
    ("counts", (WINDOW, M_DEV), F32),
    ("counts_16", (WINDOW, M_DEV), BF16),
    ("exps", (HEADS, WINDOW, M_DEV), F32),
    ("probs", (HEADS, WINDOW, M_DEV), BF16),
    ("attended", (D, M_DEV), BF16),
    ("mesh_out", (D, M_DEV), BF16),
    ("table", (WINDOW, G_DEV), BF16),
    ("vars_own", (ROWS, M_DEV), F32),
    ("vars_two", (2 * ROWS, M_DEV), BF16),
    ("vars_out", (ROWS, M_DEV), BF16),
    ("vars_in", (ROWS, 2 * M_DEV), BF16),
    ("net", (ROWS, G_DEV), F32),
    ("weights", (VARS, G_DEV), F32),
    ("grad_net", (ROWS, G_DEV), BF16),
    ("node_out", (2, ROWS, M_DEV), BF16),
    ("node_in", (2, ROWS, M_DEV), BF16),
    ("node_own", (ROWS, M_DEV), F32),
    ("mesh_grad", (D, M_DEV), BF16),
    ("head_grad", (D, M_DEV), BF16),
    ("value_out", (2, D, M_DEV), BF16),
    ("value_in", (2, D, M_DEV), BF16),
    ("value_own", (D, M_DEV), F32),
    ("part_out", (2048, 128), F32),
    ("part_value", (2048, 128), F32),
    ("part_dec", (512, 128), F32),
)


def step_kernel(level_ref, head_scale_ref, *refs):
    hbm, (total_out, total_value, total_dec) = refs[: len(INPUTS)], refs[len(INPUTS) : len(INPUTS) + 3]
    scratch = refs[len(INPUTS) + 3 :]
    send_sems, recv_sems, load_sems = scratch[:3]
    held = dict(zip([name for name, shape, kind in INPUTS + SCRATCH], scratch[3:]))
    unit_refs = scratch[3 + len(INPUTS + SCRATCH) :]
    noisy_ref, g2m_ref, embed_in_ref, embed_out_ref = [
        held[name] for name in ("noisy", "g2m", "embed_in", "embed_out")
    ]
    gain_ref, qkv_ref, nbr_ref, m2g_ref = [held[name] for name in ("gain", "qkv", "nbr", "m2g")]
    out_w_ref, dec_w_ref, target_ref, var_ref = [held[name] for name in ("out_w", "dec_w", "target", "var")]
    (
        state_in,
        g2m_in,
        pad_in,
        embed_in_t,
        dec_t,
        dec_full,
        embed_out_t,
        q_t,
        k_t,
        v_t,
        out_t,
        node_hidden,
        mesh_in,
        normed,
        normed_in,
        unit_q,
        unit_k,
        values,
        counts,
        counts_16,
        exps,
        probs,
        attended,
        mesh_out,
        table,
        vars_own,
        vars_two,
        vars_out,
        vars_in,
        net,
        weights_ref,
        grad_net,
        node_out,
        node_in,
        node_own,
        mesh_grad,
        head_grad,
        value_out,
        value_in,
        value_own,
        part_out,
        part_value,
        part_dec,
    ) = [held[name] for name, shape, kind in SCRATCH]
    parts = {"out": part_out, "value": part_value, "dec": part_dec}
    totals = {"out": total_out, "value": total_value, "dec": total_dec}
    at = coordinates()
    band = at["band"]
    left = (lax.rem(band + 15, 16), at["x"], at["core"])
    right = (lax.rem(band + 1, 16), at["x"], at["core"])
    sides = ((0, left, 1), (1, right, 0))
    base = band * M_DEV
    copies = Copies(send_sems, recv_sems)
    phase = Phase()
    phase("greet")
    partners = [left, right] + sum_partners(at)
    greet(partners)
    loads = {}
    for index, (name, shape, kind) in enumerate(INPUTS):
        source = hbm[index].at[0] if name in ("noisy", "target") else hbm[index]
        loads[name] = pltpu.make_async_copy(source, held[name], load_sems.at[index])
        loads[name].start()
    loads["noisy"].wait()
    loads["g2m"].wait()
    await_greetings(partners)

    phase("sendstate")
    node_flight = copies.start(g2m_in, [(g2m_ref, g2m_in.at[slot], device) for side, device, slot in sides])
    state_flights = []
    for chunk in range(4):
        cells = pl.ds(512 * chunk, 512)
        state_flights.append(
            copies.start(
                state_in.at[:, :, cells],
                [
                    (noisy_ref.at[:, cells], state_in.at[slot, :, cells], device)
                    for side, device, slot in sides
                ],
            )
        )

    phase("transposes")
    loads["embed_in"].wait()
    pad_in[...] = jnp.zeros_like(pad_in)
    pad_in[:VARS, :] = embed_in_ref[...]
    embed_in_t[...] = jnp.transpose(pad_in[...])
    level = jnp.full((1, 1), level_ref[0], F32)
    level_sq = level * level + 1.0
    scale_in = lax.rsqrt(level_sq)
    skip_scale = 1.0 / level_sq
    out_scale = level * scale_in
    half_scale = 0.5 * scale_in

    def encode(state, nodes):
        half_t = dot(embed_in_t[:, :VARS], state) * half_scale
        hidden = (half_t + half_t * jnp.tanh(half_t)).astype(BF16)
        ids = lax.broadcasted_iota(I32, (M_DEV, 512), 0)
        chosen = jnp.where(nodes - base == ids, 1.0, 0.0).astype(BF16)
        node_hidden[...] += dot_t(hidden, chosen)

    phase("encodeown")
    node_hidden[...] = jnp.zeros_like(node_hidden)

    @pl.loop(0, 4)
    def _(chunk):
        cells = pl.ds(pl.multiple_of(chunk * 512, 512), 512)
        encode(noisy_ref[:, cells], g2m_ref[:, cells])

    loads["embed_out"].wait()
    embed_out_t[...] = jnp.transpose(embed_out_ref[...])
    phase("encodehalo")
    node_flight.wait_recv()
    for chunk in range(4):
        cells = slice(512 * chunk, 512 * chunk + 512)
        state_flights[chunk].wait_recv()

        @pl.loop(0, 2)
        def _(slot):
            encode(state_in[slot, :, cells], g2m_in[slot, :, cells])

    phase("embedout")
    encoded = None
    for piece in pieces_of(node_hidden[...], 3):
        term = dot(embed_out_t[...], piece)
        encoded = term if encoded is None else encoded + term
    mesh_in[...] = encoded
    mean_sq = jnp.mean(encoded * encoded, axis=0, keepdims=True)
    loads["gain"].wait()
    gain = lanes(column_of(gain_ref[...], D), M_DEV)
    normed[...] = (encoded * lax.rsqrt(mean_sq + 1e-05) * gain).astype(BF16)

    normed_flights = []
    for chunk in range(4):
        nodes = pl.ds(128 * chunk, 128)
        normed_flights.append(
            copies.start(
                normed_in.at[:, pl.ds(256 * chunk, 256)],
                [
                    (normed.at[:, nodes], normed_in.at[:, pl.ds(256 * chunk + 128 * slot, 128)], device)
                    for side, device, slot in sides
                ],
            )
        )

    phase("queries")
    loads["qkv"].wait()
    q_t[...] = jnp.transpose(qkv_ref[0])
    k_t[...] = jnp.transpose(qkv_ref[1])
    v_t[...] = jnp.transpose(qkv_ref[2])
    unit_q[...] = unit_heads(dot(q_t[...], normed[...]), M_DEV).astype(BF16)

    def attend(near, start, width):
        keys = unit_heads(dot(k_t[...], near), width).astype(BF16)
        unit_k[start : start + width, :] = jnp.transpose(keys)
        values[:, start : start + width] = dot(v_t[...], near).astype(BF16)
        sums_now = []
        count = counts[start : start + width, :]
        for head in range(HEADS):
            part = slice(HEAD_DIM * head, HEAD_DIM * head + HEAD_DIM)
            scores = dot(unit_k[start : start + width, part], unit_q[part, :])
            exp = jnp.exp(scores * (head_scale_ref[head] / HEAD_DIM))
            exps[head, start : start + width, :] = exp
            sums_now.append(jnp.sum(exp * count, axis=0, keepdims=True))
        return sums_now

    phase("counts")
    loads["nbr"].wait()
    @pl.loop(0, 8)
    def _(block):
        ids = lax.broadcasted_iota(I32, (64, M_DEV), 0) + block * 64
        total = jnp.zeros((64, M_DEV), I32)
        for j in range(NBR):
            near = nbr_ref[j : j + 1, :] - (base - M_DEV)
            patch = near // M_DEV
            within = near - patch * M_DEV
            field = jnp.where(patch == 0, 64, jnp.where(patch == 1, 1, 4096))
            total = total + jnp.where(within == ids, field, 0)
        chunk = block // 2
        part = (block - 2 * chunk) * 64
        for start, shift in (
            (block * 64, 0),
            (M_DEV + 256 * chunk + part, 6),
            (M_DEV + 256 * chunk + 128 + part, 12),
        ):
            count = lax.shift_right_logical(total, jnp.full_like(total, shift)) & 63
            rows = pl.ds(pl.multiple_of(start, 64), 64)
            counts[rows, :] = count.astype(F32)
            counts_16[rows, :] = count.astype(F32).astype(BF16)

    phase("table")
    loads["m2g"].wait()
    for block in range(12):
        if block < 4:
            offset = 128 * block
        else:
            offset = 128 * ((block - 4) // 2) + (M_DEV if (block - 4) % 2 else -M_DEV)
        ids = lax.broadcasted_iota(I32, (128, G_DEV), 0) + (base + offset)
        table[128 * block : 128 * block + 128, :] = jnp.where(m2g_ref[...] == ids, 1.0, 0.0).astype(BF16)

    phase("weights")
    loads["var"].wait()
    cells = lax.broadcasted_iota(I32, (1, G_DEV), 1) + band * G_DEV
    lat_weight = 0.2 + jnp.cos(math.pi * (cells.astype(F32) + 0.5) / GRID - 0.5 * math.pi)
    square = lax.broadcasted_iota(I32, (VARS, VARS), 0) == lax.broadcasted_iota(I32, (VARS, VARS), 1)
    var_column = jnp.sum(jnp.where(square, var_ref[...], 0.0), axis=1, keepdims=True)
    weights_ref[...] = var_column * lat_weight
    loads["out_w"].wait()
    loads["dec_w"].wait()
    out_t[...] = jnp.transpose(out_w_ref[...])
    dec_t[...] = jnp.zeros_like(dec_t)
    dec_t[:VARS, :] = dec_w_ref[...]
    dec_full[...] = jnp.transpose(dec_t[...])
    loads["target"].wait()
    phase("scores")
    exp_sums = None
    for chunk in range(6):
        if chunk < 2:
            near = normed[:, 256 * chunk : 256 * chunk + 256]
        else:
            normed_flights[chunk - 2].wait_recv()
            near = normed_in[:, 256 * (chunk - 2) : 256 * (chunk - 2) + 256]
        sums_now = attend(near, 256 * chunk, 256)
        exp_sums = sums_now if exp_sums is None else [a + b for a, b in zip(exp_sums, sums_now)]

    phase("probs")
    for head in range(HEADS):
        inverse = 1.0 / exp_sums[head]
        part = slice(HEAD_DIM * head, HEAD_DIM * head + HEAD_DIM)

        @pl.loop(0, 6)
        def _(block):
            rows = pl.ds(pl.multiple_of(block * 256, 256), 256)
            prob = (exps[head, rows, :] * inverse).astype(BF16)
            probs[head, rows, :] = prob * counts_16[rows, :]

        attended[part, :] = dot(values[part, :], probs[head]).astype(BF16)

    phase("meshout")
    mesh_out[...] = (mesh_in[...] + dot(out_t[...], attended[...])).astype(BF16)
    vars_own[...] = dot(dec_t[:ROWS, :], mesh_out[...])
    vars_out[...] = vars_own[...].astype(BF16)
    vars_flight = copies.start(
        vars_in,
        [
            (
                vars_out.at[:, pl.ds(128 * chunk, 128)],
                vars_in.at[:, pl.ds(256 * chunk + 128 * slot, 128)],
                device,
            )
            for chunk in range(4)
            for side, device, slot in sides
        ],
    )

    phase("decodeown")
    for index, piece in enumerate(pieces_of(vars_own[...], 2)):
        vars_two[ROWS * index : ROWS * index + ROWS, :] = piece

    @pl.loop(0, 4)
    def _(chunk):
        cells = pl.ds(pl.multiple_of(chunk * 512, 512), 512)
        both = dot(vars_two[...], table[:M_DEV, cells])
        net[:, cells] = both[:ROWS, :] + both[ROWS:, :]

    phase("waitvars")
    vars_flight.wait_recv()
    phase("decodehalo")

    @pl.loop(0, 4)
    def _(chunk):
        cells = pl.ds(pl.multiple_of(chunk * 512, 512), 512)
        net[:, cells] = net[:, cells] + dot(vars_in[...], table[M_DEV:, cells])

    phase("errors")
    weights = weights_ref[...]
    errors = (
        skip_scale * noisy_ref[...].astype(F32) + out_scale * net[:VARS, :] - target_ref[...].astype(F32)
    )
    scale_all = 1.0 / (MEMBERS * VARS)
    loss = jnp.sum(jnp.sum(weights * errors * errors, axis=1, keepdims=True), axis=0, keepdims=True) * scale_all
    grad_net[...] = jnp.zeros_like(grad_net)
    grad_net[:VARS, :] = ((2.0 * out_scale * scale_all) * weights * errors).astype(BF16)

    phase("nodepart")
    node_part = dot_t(grad_net[...], table[M_DEV:, :])
    for chunk in range(4):
        for side in (0, 1):
            start = 256 * chunk + 128 * side
            node_out[side, :, 128 * chunk : 128 * chunk + 128] = node_part[:, start : start + 128].astype(BF16)
    node_flight = copies.start(
        node_in, [(node_out.at[side], node_in.at[slot], device) for side, device, slot in sides]
    )
    phase("nodeown")
    node_own[...] = dot_t(grad_net[...], table[:M_DEV, :])
    phase("waitnode")
    node_flight.wait_recv()
    node_grad = node_own[...] + node_in[0].astype(F32) + node_in[1].astype(F32)
    phase("meshgrad")
    node_pieces = pieces_of(node_grad, 3)
    grown = None
    for piece in node_pieces:
        term = dot(dec_full[:, :ROWS], piece)
        grown = term if grown is None else grown + term
    mesh_grad[...] = grown.astype(BF16)
    head_grad[...] = dot(out_w_ref[...], mesh_grad[...]).astype(BF16)

    phase("valuerim")
    value_flights = []
    for head in range(HEADS):
        part = slice(HEAD_DIM * head, HEAD_DIM * head + HEAD_DIM)
        spread = dot_t(head_grad[part, :], probs[head, M_DEV:, :])
        for chunk in range(4):
            for side in (0, 1):
                start = 256 * chunk + 128 * side
                value_out[side, part, 128 * chunk : 128 * chunk + 128] = spread[
                    :, start : start + 128
                ].astype(BF16)
        rows = pl.ds(HEAD_DIM * head, HEAD_DIM)
        value_flights.append(
            copies.start(
                value_in.at[:, rows, :],
                [
                    (value_out.at[side, rows, :], value_in.at[slot, rows, :], device)
                    for side, device, slot in sides
                ],
            )
        )

    phase("gradout")
    units = []
    for index, unit in enumerate(UNITS):
        name = unit[0]
        units.append(
            device_sum(parts[name], totals[name], unit, unit_refs[7 * index : 7 * index + 7], copies, at)
        )
    out_units, value_units = (units[:3], units[3:])
    out_sum = dot_t(attended[...], mesh_grad[...])
    for lane in range(4):
        part_out[512 * lane : 512 * lane + 512, :] = out_sum[:, 128 * lane : 128 * lane + 128]
    for unit in out_units[:2]:
        next(unit)
    dec_sum = None
    for piece in node_pieces:
        term = dot_t(piece, mesh_out[...])
        dec_sum = term if dec_sum is None else dec_sum + term
    for lane in range(4):
        part_dec[ROWS * lane : ROWS * lane + ROWS, :] = dec_sum[:, 128 * lane : 128 * lane + 128]
    part_dec[4 * ROWS :, :] = jnp.broadcast_to(loss, (128, 128))
    next(out_units[2])
    phase("valueown")
    for head in range(HEADS):
        part = slice(HEAD_DIM * head, HEAD_DIM * head + HEAD_DIM)
        value_own[part, :] = dot_t(head_grad[part, :], probs[head, :M_DEV, :])

    def advance(some):
        for unit in some:
            next(unit, None)

    def finish_head(head):
        phase("gradvalue%d" % head)
        part = slice(HEAD_DIM * head, HEAD_DIM * head + HEAD_DIM)
        value_flights[head].wait_recv()
        grad = value_own[part, :] + value_in[0, part, :].astype(F32) + value_in[1, part, :].astype(F32)
        part_value[512 * head : 512 * head + 512, :] = dot_t(normed[...], grad.astype(BF16))
        next(value_units[head])

    advance(out_units)
    finish_head(0)
    advance(value_units[:1])
    finish_head(1)
    advance(value_units[1:2])
    finish_head(2)
    advance(value_units[2:3])
    finish_head(3)
    advance(out_units)
    advance(value_units[3:])
    for turn in range(6):
        phase("turn%d" % turn)
        advance(value_units + out_units)
    phase("drain")
    for copy in copies.all:
        copy.wait_send()
    phase(None)


def finish_kernel(out_ref, value_ref, dec_ref, out_hbm, value_hbm, dec_result, loss_result, sems):
    flights = []
    for index, (source, target) in enumerate(((out_ref, out_hbm), (value_ref, value_hbm))):
        for lane in range(4):
            flights.append(
                pltpu.make_async_copy(
                    source.at[pl.ds(512 * lane, 512), :],
                    target.at[:, pl.ds(128 * lane, 128)],
                    sems.at[4 * index + lane],
                )
            )
            flights[-1].start()
    for lane in range(4):
        dec_result[:, 128 * lane : 128 * lane + 128] = dec_ref[ROWS * lane : ROWS * lane + VARS, :]
    loss_result[...] = dec_ref[4 * ROWS : 4 * ROWS + 1, :1] / GRID
    for flight in flights:
        flight.wait()


def local(
    noisy_state,
    target_state,
    noise_level,
    var_weight,
    embed_in,
    embed_out,
    norm_gain,
    qkv_weight,
    head_scale,
    out_weight,
    dec_weight,
    g2m_node,
    m2g_node,
    neighbours,
):
    vmem = pl.BlockSpec(memory_space=pltpu.VMEM)
    smem = pl.BlockSpec(memory_space=pltpu.SMEM)
    anywhere = pl.BlockSpec(memory_space=pl.ANY)
    copies = 15 + 7 * len(UNITS)
    scratch = [pltpu.SemaphoreType.DMA((copies,))] * 2 + [pltpu.SemaphoreType.DMA((len(INPUTS),))]
    scratch += [pltpu.VMEM(shape, kind) for name, shape, kind in INPUTS + SCRATCH]
    for unit in UNITS:
        scratch += sum_scratch(unit[2])
    totals = pl.pallas_call(
        step_kernel,
        out_shape=[pltpu.VMEM((rows, 128), F32) for rows in (2048, 2048, 512)],
        in_specs=[smem, smem] + [anywhere] * len(INPUTS),
        out_specs=[vmem] * 3,
        scratch_shapes=scratch,
        compiler_params=pltpu.CompilerParams(
            collective_id=0, has_side_effects=True, vmem_limit_bytes=STEP_VMEM
        ),
        name="step",
    )(
        noise_level,
        head_scale,
        noisy_state,
        g2m_node.reshape(1, G_DEV),
        embed_in,
        embed_out,
        norm_gain.reshape(1, D),
        qkv_weight,
        neighbours.T,
        m2g_node.reshape(1, G_DEV),
        out_weight,
        dec_weight.T,
        target_state,
        var_weight.reshape(1, VARS),
    )
    square = jax.ShapeDtypeStruct((D, D), F32)
    grad_out, grad_value, dec, loss = pl.pallas_call(
        finish_kernel,
        out_shape=(square, square, jax.ShapeDtypeStruct((VARS, D), F32), jax.ShapeDtypeStruct((1, 1), F32)),
        in_specs=[vmem] * 3,
        out_specs=(anywhere, anywhere, vmem, vmem),
        scratch_shapes=[pltpu.SemaphoreType.DMA((8,))],
        compiler_params=pltpu.CompilerParams(vmem_limit_bytes=8 << 20),
        name="finish",
    )(*totals)
    return loss.reshape(()), dec.T, grad_out, grad_value


def solution(mesh):
    in_specs = (
        P(("chan", "member"), None, "band"),
        P(("chan", "member"), None, "band"),
        P(("chan", "member")),
        P(),
        P(),
        P(),
        P(),
        P(),
        P(),
        P(),
        P(),
        P("band"),
        P("band"),
        P("band", None),
    )
    out_specs = (P(), P(), P(), P())
    return jax.shard_map(local, mesh=mesh, in_specs=in_specs, out_specs=out_specs, check_vma=False)
```

time: 122 us -> 96.8 us (0.79)
  Pallas kernels: 109 us -> 95.2 us
  local copies, waits for them, and re-layouts: 8.01 us -> 0 us
  between operations: 3.08 us -> 1.45 us
    pallas_call x1 -> x2, Pallas kernels: 109 us -> 95.2 us  [the longest x1 93.1 us: local(): pl.pallas_call(step_kernel, out_shape=[pltpu.VMEM((rows, 128), F32) for r...]
    unnamed x6 -> x0, local copies, waits for them, and re-layouts: 6.75 us -> none
    slice x1 -> x0, local copies, waits for them, and re-layouts: 1.26 us -> none  [local(): return (dec[0, 127] / GRID, dec[:, :VARS], grad_out, grad_value)]
where the time goes in v2:
time: 96.8 us; the launch traced here: 96.6 us
  Pallas kernels  95.2 us (98%)
  between operations  1.45 us (1%)
    pallas_call x1, Pallas kernels, local(): pl.pallas_call(step_kernel, out_shape=[pltpu.VMEM((rows, 128), F32) for r...  93.1 us
    pallas_call x1, Pallas kernels, local(): pl.pallas_call(finish_kernel, out_shape=(square, square, jax.ShapeDtypeSt...  2.05 us

profile of v2, /device:TPU:1, one launch (start us, length us, event | category | flops | bytes accessed | tf_op | source)
XLA Modules:
  0.0 96.6 jit_solution(4194524106894065895)
XLA Ops:
  1.3 93.1 %step.1 = (f32[2048,128]{1,0:T(8,128)S(1)}, f32[2048,128]{1,0:T(8,128)S(1)}, f32[512,128]{1,0:T(8,128)S(1)}) custom-call(f32[1]{0:T(128)S(6)} %copy.18.level_ref, f32[4]{0:T(128)} %head_scale_ref.1, bf16[1,84,2048]{2,1,0:T(8,128)(2,1)} %refs_0_.1, s32[1,2048]{1,0:T(1,128)} %bitcast.10, bf16[84,512]{1,0:T(8,128)(2,1)} %refs_2_.1, bf16[512,512]{1,0:T(8,128)(2,1)} %refs_3_.1, ...), custom_call_target="tpu_custom_call" | custom-call | tf_op jit(solution)/shard_map/step/pallas_call | solution.py:727
  94.4 2.1 %finish.1 = (f32[512,512]{1,0:T(8,128)}, f32[512,512]{1,0:T(8,128)}, f32[84,512]{1,0:T(8,128)}, f32[1,1]{1,0:T(1,128)}) custom-call(f32[2048,128]{1,0:T(8,128)S(1)} %get-tuple-element.11.out_ref, f32[2048,128]{1,0:T(8,128)S(1)} %get-tuple-element.12.value_ref, f32[512,128]{1,0:T(8,128)S(1)} %get-tuple-element.13.dec_ref), custom_call_target="tpu_custom_call" | custom-call | tf_op jit(solution)/shard_map/finish/pallas_call | solution.py:754

commit v3 on v2

v3 whole, which is shorter than its diff:
```python
import math

import jax
import jax.numpy as jnp
from jax import lax
from jax.experimental import pallas as pl
from jax.experimental.pallas import tpu as pltpu
from jax.sharding import PartitionSpec as P

D = 512
VARS = 84
HEADS = 4
NBR = 32
G_DEV = 2048
M_DEV = 512
HEAD_DIM = 128
GRID = 32768
MEMBERS = 8
WINDOW = 3 * M_DEV
ROWS = 96
BF16, F32, I32 = jnp.bfloat16, jnp.float32, jnp.int32
MESH_ID = pl.DeviceIdType.MESH
UNITS = (
    (0, 0, 768, 0, 0, "xyz"),
    (0, 768, 768, 0, 1, "yzx"),
    (0, 1536, 512, 1, 0, "zxy"),
    (2, 0, 512, 4, 0, "zxy"),
    (1, 0, 768, 2, 0, "xyz"),
    (1, 768, 768, 2, 1, "yzx"),
    (1, 1536, 512, 3, 0, "zxy"),
)
TOTALS = ((4, 4, 96, 128), (2, 4, 64, 128), (4, 4, 96, 128), (2, 4, 64, 128), (2, 4, 64, 128))


def coordinates():
    band, chan, core = (lax.axis_index("band"), lax.axis_index("chan"), lax.axis_index("member"))
    return {"band": band, "x": chan, "y": lax.rem(band, 4), "z": band // 4, "core": core}


def peer_on(axis, at, step):
    other = lax.rem(at[axis] + step, 4)
    if axis == "x":
        return (at["band"], other, at["core"])
    if axis == "y":
        return (at["z"] * 4 + other, at["x"], at["core"])
    return (other * 4 + at["y"], at["x"], at["core"])


def sibling(at):
    return (at["band"], at["x"], 1 - at["core"])


class Flight:
    def __init__(self, copies, index, size_ref, device):
        self.whole = pltpu.make_async_remote_copy(
            src_ref=size_ref,
            dst_ref=size_ref,
            send_sem=copies.send_sems.at[index],
            recv_sem=copies.recv_sems.at[index],
            device_id=device,
            device_id_type=MESH_ID,
        )

    def wait_recv(self):
        self.whole.wait_recv()

    def wait_send(self):
        self.whole.wait_send()


class Copies:
    def __init__(self, send_sems, recv_sems):
        self.send_sems, self.recv_sems, self.all = send_sems, recv_sems, []

    def start(self, size_ref, group):
        index = len(self.all)
        for source, target, device in group:
            pltpu.make_async_remote_copy(
                src_ref=source,
                dst_ref=target,
                send_sem=self.send_sems.at[index],
                recv_sem=self.recv_sems.at[index],
                device_id=device,
                device_id_type=MESH_ID,
            ).start()
        self.all.append(Flight(self, index, size_ref, group[0][2]))
        return self.all[-1]


def greet(devices):
    for device in devices:
        pl.semaphore_signal(
            pltpu.get_barrier_semaphore(), inc=1, device_id=device, device_id_type=MESH_ID
        )


def await_greetings(devices):
    pl.semaphore_wait(pltpu.get_barrier_semaphore(), len(devices))


def sum_partners(at):
    return [sibling(at)] + [peer_on(axis, at, step) for axis in ("x", "y", "z") for step in (1, 2, 3)]


def sum_scratch(rows):
    half = rows // 2
    return [
        pltpu.VMEM((half, 128), F32),
        pltpu.VMEM((half, 128), F32),
        pltpu.VMEM((3, half // 4, 128), F32),
        pltpu.VMEM((half // 4, 128), F32),
        pltpu.VMEM((3, half // 16, 128), F32),
        pltpu.VMEM((4, half // 16, 128), F32),
        pltpu.VMEM((half // 16, 128), F32),
    ]


def device_sum(part, total, unit, refs, copies, at):
    near, pair, first_in, first, second_in, slots, second = refs
    origin, size_all, which, place, (first_axis, second_axis, third_axis) = unit[1:]
    half = size_all // 2
    quarter, tiny = half // 4, half // 16

    def rows(start, size):
        return pl.ds(pl.multiple_of(start, size), size)

    def scatter(source, landing, size, axis):
        group = []
        for step in (1, 2, 3):
            block = source.at[rows(lax.rem(at[axis] + step, 4) * size, size), :]
            group.append((block, landing.at[step - 1], peer_on(axis, at, step)))
        return copies.start(landing, group)

    def gather_sum(source, landing, size, axis, flight):
        flight.wait_recv()
        return (source[rows(at[axis] * size, size), :] + landing[0]) + (landing[1] + landing[2])

    mine = origin + at["core"] * half
    flight = copies.start(
        near, [(part.at[rows(origin + (1 - at["core"]) * half, half), :], near, sibling(at))]
    )
    yield
    flight.wait_recv()
    pair[...] = part[rows(mine, half), :] + near[...]
    flight = scatter(pair, first_in, quarter, first_axis)
    yield
    first[...] = gather_sum(pair, first_in, quarter, first_axis, flight)
    flight = scatter(first, second_in, tiny, second_axis)
    yield
    second[...] = gather_sum(first, second_in, tiny, second_axis, flight)
    slots[at[third_axis]] = second[...]
    flight = copies.start(
        slots.at[pl.ds(0, 3)],
        [(second, slots.at[at[third_axis]], peer_on(third_axis, at, step)) for step in (1, 2, 3)],
    )
    yield
    flight.wait_recv()
    block = 2 * place + at["core"]
    one = total.at[block, at[first_axis], rows(at[second_axis] * tiny, tiny), :]
    total[block, at[first_axis], rows(at[second_axis] * tiny, tiny), :] = (slots[0] + slots[1]) + (
        slots[2] + slots[3]
    )
    flight = copies.start(
        total.at[block, pl.ds(0, 3), rows(0, tiny), :],
        [(one, one, peer_on(first_axis, at, step)) for step in (1, 2, 3)],
    )
    yield
    flight.wait_recv()
    line = total.at[block, :, rows(at[second_axis] * tiny, tiny), :]
    flight = copies.start(
        total.at[block, :, pl.ds(0, 3 * tiny), :],
        [(line, line, peer_on(second_axis, at, step)) for step in (1, 2, 3)],
    )
    yield
    flight.wait_recv()
    flight = copies.start(total.at[block], [(total.at[block], total.at[block], sibling(at))])
    yield
    flight.wait_recv()
    yield


def dot(left, right):
    return jnp.dot(left, right, preferred_element_type=F32)


def dot_t(left, right):
    return lax.dot_general(left, right, (((1,), (1,)), ((), ())), preferred_element_type=F32)


def pieces_of(values, count):
    pieces, rest = ([], values)
    for index in range(count):
        piece = rest.astype(BF16)
        pieces.append(piece)
        if index + 1 < count:
            rest = rest - piece.astype(F32)
    return pieces


def column_of(row, size):
    tall = jnp.transpose(jnp.broadcast_to(row, (128, size)))
    return tall


def unit_heads(values, width):
    split = values.reshape(HEADS, HEAD_DIM, width)
    scale = lax.rsqrt(jnp.mean(split * split, axis=1, keepdims=True) + 1e-06)
    return (split * scale).reshape(D, width)


def lanes(values, width):
    return jnp.concatenate([values] * (width // 128), axis=1)


STEP_VMEM = 59 << 20
CHUNKS = ((0, 512), (512, 512), (1024, 512), (1536, 256), (1792, 256))
INPUTS = (
    ("noisy", (VARS, G_DEV), BF16),
    ("g2m", (1, G_DEV), I32),
    ("embed_in", (VARS, D), BF16),
    ("embed_out", (D, D), BF16),
    ("gain", (1, D), F32),
    ("qkv", (3, D, D), BF16),
    ("nbr", (NBR, M_DEV), I32),
    ("m2g", (1, G_DEV), I32),
    ("out_w", (D, D), BF16),
    ("dec_w", (VARS, D), BF16),
    ("target", (VARS, G_DEV), BF16),
    ("var", (1, VARS), F32),
    ("level", (1, 1), F32),
)

SCRATCH = (
    ((2, VARS, G_DEV), BF16),
    ((2, VARS, G_DEV), BF16),
    ((2, 1, G_DEV), I32),
    ((2, 1, G_DEV), I32),
    ((128, D), BF16),
    ((D, 128), BF16),
    ((128, D), BF16),
    ((D, 128), BF16),
    ((D, D), BF16),
    ((D, D), BF16),
    ((D, D), BF16),
    ((D, D), BF16),
    ((D, D), BF16),
    ((D, M_DEV), F32),
    ((D, M_DEV), F32),
    ((D, M_DEV), BF16),
    ((D, 2 * M_DEV), BF16),
    ((D, M_DEV), BF16),
    ((WINDOW, D), BF16),
    ((D, WINDOW), BF16),
    ((NBR, M_DEV), I32),
    ((NBR, M_DEV), I32),
    ((WINDOW, M_DEV), F32),
    ((WINDOW, M_DEV), BF16),
    ((HEADS, WINDOW, M_DEV), F32),
    ((HEADS, WINDOW, M_DEV), BF16),
    ((D, M_DEV), BF16),
    ((D, M_DEV), BF16),
    ((M_DEV, 3 * G_DEV), BF16),
    ((2 * ROWS, M_DEV), BF16),
    ((VARS, 3 * G_DEV), F32),
    ((ROWS, 3 * G_DEV), BF16),
    ((D, M_DEV), BF16),
    ((D, M_DEV), BF16),
    ((2048, 128), F32),
    ((2048, 128), F32),
    ((512, 128), F32),
)


def step_kernel(head_scale_ref, *refs):
    hbm, totals = refs[: len(INPUTS)], refs[len(INPUTS) : len(INPUTS) + len(TOTALS)]
    scratch = refs[len(INPUTS) + len(TOTALS) :]
    send_sems, recv_sems, load_sems = scratch[:3]
    held = dict(zip([name for name, shape, kind in INPUTS], scratch[3:]))
    unit_refs = scratch[3 + len(INPUTS + SCRATCH) :]
    (
        noisy_ref,
        g2m_ref,
        embed_in_ref,
        embed_out_ref,
        gain_ref,
        qkv_ref,
        nbr_ref,
        m2g_ref,
        out_w_ref,
        dec_w_ref,
        target_ref,
        var_ref,
        level_ref,
    ) = scratch[3 : 3 + len(INPUTS)]
    (
        state_in,
        target_in,
        g2m_in,
        m2g_in,
        pad_in,
        embed_in_t,
        dec_t,
        dec_full,
        embed_out_t,
        q_t,
        k_t,
        v_t,
        out_t,
        node_hidden,
        mesh_in,
        normed,
        normed_in,
        unit_q,
        unit_k,
        values,
        within,
        fields,
        counts,
        counts_16,
        exps,
        probs,
        attended,
        mesh_out,
        table,
        vars_two,
        weights_ref,
        grad_net,
        mesh_grad,
        head_grad,
        part_out,
        part_value,
        part_dec,
    ) = scratch[3 + len(INPUTS) : 3 + len(INPUTS + SCRATCH)]
    parts = (part_out, part_value, part_dec)
    at = coordinates()
    band = at["band"]
    left = (lax.rem(band + 15, 16), at["x"], at["core"])
    right = (lax.rem(band + 1, 16), at["x"], at["core"])
    sides = ((0, left, 1), (1, right, 0))
    base = band * M_DEV
    copies = Copies(send_sems, recv_sems)
    partners = [left, right] + sum_partners(at)
    greet(partners)
    loads = {}
    for index, (name, shape, kind) in enumerate(INPUTS):
        source = hbm[index].at[0] if name in ("noisy", "target") else hbm[index]
        loads[name] = pltpu.make_async_copy(source, held[name], load_sems.at[index])
        loads[name].start()
    loads["noisy"].wait()
    loads["g2m"].wait()
    await_greetings(partners)

    node_flight = copies.start(g2m_in, [(g2m_ref, g2m_in.at[slot], device) for side, device, slot in sides])
    state_flights = []
    for first, size in CHUNKS:
        cells = pl.ds(first, size)
        state_flights.append(
            copies.start(
                state_in.at[:, :, cells],
                [
                    (noisy_ref.at[:, cells], state_in.at[slot, :, cells], device)
                    for side, device, slot in sides
                ],
            )
        )


    def send_target(first, size):
        cells = pl.ds(first, size)
        return copies.start(
            target_in.at[:, :, cells],
            [(target_ref.at[:, cells], target_in.at[slot, :, cells], device) for side, device, slot in sides],
        )

    loads["m2g"].wait()
    cell_flight = copies.start(m2g_in, [(m2g_ref, m2g_in.at[slot], device) for side, device, slot in sides])
    loads["target"].wait()
    target_flights = [send_target(512 * chunk, 512) for chunk in range(3)]
    loads["embed_in"].wait()
    pad_in[...] = jnp.zeros_like(pad_in)
    pad_in[:VARS, :] = embed_in_ref[...]
    embed_in_t[...] = jnp.transpose(pad_in[...])
    loads["level"].wait()
    level = level_ref[...]
    level_sq = level * level + 1.0
    scale_in = lax.rsqrt(level_sq)
    skip_scale = 1.0 / level_sq
    out_scale = level * scale_in
    half_scale = 0.5 * scale_in

    def encode(state, nodes):
        half_t = dot(embed_in_t[:, :VARS], state) * half_scale
        hidden = (half_t + half_t * jnp.tanh(half_t)).astype(BF16)
        ids = lax.broadcasted_iota(I32, (M_DEV, state.shape[1]), 0)
        chosen = jnp.where(nodes - base == ids, 1.0, 0.0).astype(BF16)
        node_hidden[...] += dot_t(hidden, chosen)

    node_hidden[...] = jnp.zeros_like(node_hidden)

    @pl.loop(0, 4)
    def _(chunk):
        cells = pl.ds(pl.multiple_of(chunk * 512, 512), 512)
        encode(noisy_ref[:, cells], g2m_ref[:, cells])

    loads["embed_out"].wait()
    embed_out_t[...] = jnp.transpose(embed_out_ref[...])
    loads["var"].wait()
    square = lax.broadcasted_iota(I32, (VARS, VARS), 0) == lax.broadcasted_iota(I32, (VARS, VARS), 1)
    var_column = jnp.sum(jnp.where(square, var_ref[...], 0.0), axis=1, keepdims=True)

    def prepare(place, nodes):
        local = nodes - base
        ids = lax.broadcasted_iota(I32, (M_DEV, G_DEV), 0)
        block = slice(G_DEV * place, G_DEV * place + G_DEV)
        table[:, block] = jnp.where(local == ids, 1.0, 0.0).astype(BF16)
        cells = lax.broadcasted_iota(I32, (1, G_DEV), 1) + lax.rem(band + (0, 15, 1)[place], 16) * G_DEV
        lat_weight = 0.2 + jnp.cos(math.pi * (cells.astype(F32) + 0.5) / GRID - 0.5 * math.pi)
        mine = (local >= 0) & (local < M_DEV)
        weights_ref[:, block] = var_column * jnp.where(mine, lat_weight, 0.0)

    prepare(0, m2g_ref[...])
    node_flight.wait_recv()
    for (first, size), flight in zip(CHUNKS, state_flights):
        cells = slice(first, first + size)
        flight.wait_recv()

        for slot in range(2):
            encode(state_in[slot, :, cells], g2m_in[slot, :, cells])

    encoded = None
    for piece in pieces_of(node_hidden[...], 3):
        term = dot(embed_out_t[...], piece)
        encoded = term if encoded is None else encoded + term
    mesh_in[...] = encoded
    mean_sq = jnp.mean(encoded * encoded, axis=0, keepdims=True)
    loads["gain"].wait()
    gain = lanes(column_of(gain_ref[...], D), M_DEV)
    normed[...] = (encoded * lax.rsqrt(mean_sq + 1e-05) * gain).astype(BF16)

    normed_flights = []
    for chunk in range(4):
        nodes = pl.ds(128 * chunk, 128)
        normed_flights.append(
            copies.start(
                normed_in.at[:, pl.ds(256 * chunk, 256)],
                [
                    (normed.at[:, nodes], normed_in.at[:, pl.ds(256 * chunk + 128 * slot, 128)], device)
                    for side, device, slot in sides
                ],
            )
        )

    target_flights.append(send_target(1536, 512))

    loads["qkv"].wait()
    q_t[...] = jnp.transpose(qkv_ref[0])
    k_t[...] = jnp.transpose(qkv_ref[1])
    v_t[...] = jnp.transpose(qkv_ref[2])
    unit_q[...] = unit_heads(dot(q_t[...], normed[...]), M_DEV).astype(BF16)

    def attend(near, start, width):
        keys = unit_heads(dot(k_t[...], near), width).astype(BF16)
        unit_k[start : start + width, :] = jnp.transpose(keys)
        values[:, start : start + width] = dot(v_t[...], near).astype(BF16)
        sums_now = []
        count = counts[start : start + width, :]
        for head in range(HEADS):
            part = slice(HEAD_DIM * head, HEAD_DIM * head + HEAD_DIM)
            scores = dot(unit_k[start : start + width, part], unit_q[part, :])
            exp = jnp.exp(scores * (head_scale_ref[head] / HEAD_DIM))
            exps[head, start : start + width, :] = exp
            sums_now.append(jnp.sum(exp * count, axis=0, keepdims=True))
        return sums_now

    loads["nbr"].wait()
    window = nbr_ref[...] - (base - M_DEV)
    patch = lax.shift_right_arithmetic(window, jnp.full_like(window, 9))
    within[...] = window - patch * M_DEV
    fields[...] = jnp.where(patch == 0, 64, jnp.where(patch == 1, 1, 4096))

    @pl.loop(0, 8)
    def _(block):
        ids = lax.broadcasted_iota(I32, (64, M_DEV), 0) + block * 64
        total = jnp.zeros((64, M_DEV), I32)
        for j in range(NBR):
            total = total + jnp.where(within[j : j + 1, :] == ids, fields[j : j + 1, :], 0)
        chunk = block // 2
        part = (block - 2 * chunk) * 64
        for start, shift in (
            (block * 64, 0),
            (M_DEV + 256 * chunk + part, 6),
            (M_DEV + 256 * chunk + 128 + part, 12),
        ):
            count = lax.shift_right_logical(total, jnp.full_like(total, shift)) & 63
            rows = pl.ds(pl.multiple_of(start, 64), 64)
            counts[rows, :] = count.astype(F32)
            counts_16[rows, :] = count.astype(F32).astype(BF16)

    cell_flight.wait_recv()
    for slot in range(2):
        prepare(1 + slot, m2g_in[slot])

    loads["out_w"].wait()
    loads["dec_w"].wait()
    out_t[...] = jnp.transpose(out_w_ref[...])
    dec_t[...] = jnp.zeros_like(dec_t)
    dec_t[:VARS, :] = dec_w_ref[...]
    dec_full[...] = jnp.transpose(dec_t[...])
    exp_sums = None
    for chunk in range(6):
        if chunk < 2:
            near = normed[:, 256 * chunk : 256 * chunk + 256]
        else:
            normed_flights[chunk - 2].wait_recv()
            near = normed_in[:, 256 * (chunk - 2) : 256 * (chunk - 2) + 256]
        sums_now = attend(near, 256 * chunk, 256)
        exp_sums = sums_now if exp_sums is None else [a + b for a, b in zip(exp_sums, sums_now)]

    for head in range(HEADS):
        inverse = 1.0 / exp_sums[head]
        part = slice(HEAD_DIM * head, HEAD_DIM * head + HEAD_DIM)

        probs[head] = (exps[head] * inverse).astype(BF16) * counts_16[...]
        attended[part, :] = dot(values[part, :], probs[head]).astype(BF16)

    mesh_out[...] = (mesh_in[...] + dot(out_t[...], attended[...])).astype(BF16)
    for index, piece in enumerate(pieces_of(dot(dec_t[:ROWS, :], mesh_out[...]), 2)):
        vars_two[ROWS * index : ROWS * index + ROWS, :] = piece
    for flight in target_flights:
        flight.wait_recv()

    scale_all = 1.0 / (MEMBERS * VARS)
    grad_scale = 2.0 * out_scale * scale_all
    grad_net[VARS:, :] = jnp.zeros((ROWS - VARS, 3 * G_DEV), BF16)
    loss_row = jnp.zeros((1, 512), F32)
    sources = ((noisy_ref, target_ref), (state_in.at[0], target_in.at[0]), (state_in.at[1], target_in.at[1]))
    for place, (state, target) in enumerate(sources):
        for chunk in range(4):
            cells = slice(512 * chunk, 512 * chunk + 512)
            block = slice(G_DEV * place + 512 * chunk, G_DEV * place + 512 * chunk + 512)
            both = dot(vars_two[...], table[:, block])
            net = both[:VARS, :] + both[ROWS : ROWS + VARS, :]
            weights = weights_ref[:, block]
            errors = skip_scale * state[:, cells].astype(F32) + out_scale * net - target[:, cells].astype(F32)
            weighted = weights * errors
            loss_row = loss_row + jnp.sum(weighted * errors, axis=0, keepdims=True)
            grad_net[:VARS, block] = (grad_scale * weights * errors).astype(BF16)
    loss = jnp.sum(loss_row, axis=1, keepdims=True) * scale_all
    node_grad = dot_t(grad_net[...], table[...])
    node_pieces = pieces_of(node_grad, 3)
    grown = None
    for piece in node_pieces:
        term = dot(dec_full[:, :ROWS], piece)
        grown = term if grown is None else grown + term
    mesh_grad[...] = grown.astype(BF16)
    head_grad[...] = dot(out_w_ref[...], mesh_grad[...]).astype(BF16)

    units = []
    for index, unit in enumerate(UNITS):
        units.append(
            device_sum(parts[unit[0]], totals[unit[3]], unit, unit_refs[7 * index : 7 * index + 7], copies, at)
        )
    out_units, value_units = (units[:4], units[4:])
    out_sum = dot_t(attended[...], mesh_grad[...])
    for lane in range(4):
        part_out[512 * lane : 512 * lane + 512, :] = out_sum[:, 128 * lane : 128 * lane + 128]
    for unit in out_units[:3]:
        next(unit)
    dec_sum = None
    for piece in node_pieces:
        term = dot_t(piece, mesh_out[...])
        dec_sum = term if dec_sum is None else dec_sum + term
    for lane in range(4):
        part_dec[ROWS * lane : ROWS * lane + ROWS, :] = dec_sum[:, 128 * lane : 128 * lane + 128]
    part_dec[4 * ROWS :, :] = jnp.broadcast_to(loss, (128, 128))
    next(out_units[3])
    def advance(some):
        for unit in some:
            next(unit)

    for head in range(HEADS):
        part = slice(HEAD_DIM * head, HEAD_DIM * head + HEAD_DIM)
        spread = dot_t(head_grad[part, :], probs[head]).astype(BF16)
        part_value[512 * head : 512 * head + 512, :] = dot_t(normed[...], spread[:, :M_DEV]) + dot_t(
            normed_in[...], spread[:, M_DEV:]
        )
        if head == 1:
            advance(out_units)
        if head >= 1:
            next(value_units[head - 1])
        if head >= 2:
            next(value_units[head - 2])
    order = ((value_units[2:],),) + ((out_units, value_units),) * 6
    for groups in order:
        for group in groups:
            advance(group)
    assert [next(unit, "end") for unit in units] == ["end"] * len(units)
    for copy in copies.all:
        copy.wait_send()


def finish_kernel(
    out_a, out_b, value_a, value_b, dec_ref, out_hbm, value_hbm, dec_result, loss_result, sems
):
    flights = []
    for index, (source, tail, target) in enumerate(((out_a, out_b, out_hbm), (value_a, value_b, value_hbm))):
        for lane in range(4):
            flights.append(
                pltpu.make_async_copy(
                    source.at[pl.ds(512 * lane, 512), :] if lane < 3 else tail,
                    target.at[:, pl.ds(128 * lane, 128)],
                    sems.at[4 * index + lane],
                )
            )
            flights[-1].start()
    for lane in range(4):
        dec_result[:, 128 * lane : 128 * lane + 128] = dec_ref[ROWS * lane : ROWS * lane + VARS, :]
    loss_result[...] = dec_ref[4 * ROWS : 4 * ROWS + 1, :1] / GRID
    for flight in flights:
        flight.wait()


def local(
    noisy_state,
    target_state,
    noise_level,
    var_weight,
    embed_in,
    embed_out,
    norm_gain,
    qkv_weight,
    head_scale,
    out_weight,
    dec_weight,
    g2m_node,
    m2g_node,
    neighbours,
):
    vmem = pl.BlockSpec(memory_space=pltpu.VMEM)
    smem = pl.BlockSpec(memory_space=pltpu.SMEM)
    anywhere = pl.BlockSpec(memory_space=pl.ANY)
    copies = 15 + 7 * len(UNITS)
    scratch = [pltpu.SemaphoreType.DMA((copies,))] * 2 + [pltpu.SemaphoreType.DMA((len(INPUTS),))]
    scratch += [pltpu.VMEM(entry[-2], entry[-1]) for entry in INPUTS + SCRATCH]
    for unit in UNITS:
        scratch += sum_scratch(unit[2])
    totals = pl.pallas_call(
        step_kernel,
        out_shape=[pltpu.VMEM(shape, F32) for shape in TOTALS],
        in_specs=[smem] + [anywhere] * len(INPUTS),
        out_specs=[vmem] * len(TOTALS),
        scratch_shapes=scratch,
        compiler_params=pltpu.CompilerParams(
            collective_id=0, has_side_effects=True, vmem_limit_bytes=STEP_VMEM
        ),
        name="step",
    )(
        head_scale,
        noisy_state,
        g2m_node.reshape(1, G_DEV),
        embed_in,
        embed_out,
        norm_gain.reshape(1, D),
        qkv_weight,
        neighbours.T,
        m2g_node.reshape(1, G_DEV),
        out_weight,
        dec_weight.T,
        target_state,
        var_weight.reshape(1, VARS),
        noise_level.reshape(1, 1),
    )
    square = jax.ShapeDtypeStruct((D, D), F32)
    grad_out, grad_value, dec, loss = pl.pallas_call(
        finish_kernel,
        out_shape=(square, square, jax.ShapeDtypeStruct((VARS, D), F32), jax.ShapeDtypeStruct((1, 1), F32)),
        in_specs=[vmem] * len(TOTALS),
        out_specs=(anywhere, anywhere, vmem, vmem),
        scratch_shapes=[pltpu.SemaphoreType.DMA((8,))],
        compiler_params=pltpu.CompilerParams(vmem_limit_bytes=8 << 20),
        name="finish",
    )(*[total.reshape(-1, 128) for total in totals])
    return loss.reshape(()), dec.T, grad_out, grad_value


def solution(mesh):
    in_specs = (
        P(("chan", "member"), None, "band"),
        P(("chan", "member"), None, "band"),
        P(("chan", "member")),
        P(),
        P(),
        P(),
        P(),
        P(),
        P(),
        P(),
        P(),
        P("band"),
        P("band"),
        P("band", None),
    )
    out_specs = (P(), P(), P(), P())
    return jax.shard_map(local, mesh=mesh, in_specs=in_specs, out_specs=out_specs, check_vma=False)
```

time: 96.8 us -> 78.3 us (0.81)
  Pallas kernels: 95.2 us -> 76.7 us
    pallas_call x1, Pallas kernels: 93.1 us -> 74.6 us  [local(): pl.pallas_call(step_kernel, out_shape=[pltpu.VMEM(shape, F32) for shape i...]
where the time goes in v3:
time: 78.3 us; the launch traced here: 78.1 us
  Pallas kernels  76.7 us (98%)
  between operations  1.47 us (2%)
    pallas_call x1, Pallas kernels, local(): pl.pallas_call(step_kernel, out_shape=[pltpu.VMEM(shape, F32) for shape i...  74.6 us
    pallas_call x1, Pallas kernels, local(): pl.pallas_call(finish_kernel, out_shape=(square, square, jax.ShapeDtypeSt...  2.05 us

profile of v3, /device:TPU:1, one launch (start us, length us, event | category | flops | bytes accessed | tf_op | source)
XLA Modules:
  0.0 78.1 jit_solution(4930554776344541844)
XLA Ops:
  1.3 74.6 %step.1 = (f32[4,4,96,128]{3,2,1,0:T(8,128)S(1)}, f32[2,4,64,128]{3,2,1,0:T(8,128)S(1)}, f32[4,4,96,128]{3,2,1,0:T(8,128)S(1)}, f32[2,4,64,128]{3,2,1,0:T(8,128)S(1)}, f32[2,4,64,128]{3,2,1,0:T(8,128)S(1)}) custom-call(f32[4]{0:T(128)} %head_scale_ref.1, bf16[1,84,2048]{2,1,0:T(8,128)(2,1)} %refs_0_.1, s32[1,2048]{1,0:T(1,128)} %bitcast.22, ...), custom_call_target="tpu_custom_call" | custom-call | tf_op jit(solution)/shard_map/step/pallas_call | solution.py:647
  75.9 2.1 %finish.1 = (f32[512,512]{1,0:T(8,128)}, f32[512,512]{1,0:T(8,128)}, f32[84,512]{1,0:T(8,128)}, f32[1,1]{1,0:T(1,128)}) custom-call(f32[1536,128]{1,0:T(8,128)S(1)} %bitcast.15, f32[512,128]{1,0:T(8,128)S(1)} %bitcast.17, f32[1536,128]{1,0:T(8,128)S(1)} %bitcast.16, f32[512,128]{1,0:T(8,128)S(1)} %bitcast.18, f32[512,128]{1,0:T(8,128)S(1)} %bitcast.19), custom_call_target="tpu_custom_call" | custom-call | tf_op jit(solution)/shard_map/finish/pallas_call | solution.py:674

commit v4 on v3

--- a/solution.py
+++ b/solution.py
@@ -23,13 +23,12 @@
 UNITS = (
     (0, 0, 768, 0, 0, "xyz"),
     (0, 768, 768, 0, 1, "yzx"),
-    (0, 1536, 512, 1, 0, "zxy"),
-    (2, 0, 512, 4, 0, "zxy"),
+    (0, 1536, 1024, 1, 0, "zxy"),
     (1, 0, 768, 2, 0, "xyz"),
     (1, 768, 768, 2, 1, "yzx"),
     (1, 1536, 512, 3, 0, "zxy"),
 )
-TOTALS = ((4, 4, 96, 128), (2, 4, 64, 128), (4, 4, 96, 128), (2, 4, 64, 128), (2, 4, 64, 128))
+TOTALS = ((4, 4, 96, 128), (2, 4, 128, 128), (4, 4, 96, 128), (2, 4, 64, 128))
 
 
 def coordinates():
@@ -52,6 +51,7 @@
 
 class Flight:
     def __init__(self, copies, index, size_ref, device):
+        self.index = index
         self.whole = pltpu.make_async_remote_copy(
             src_ref=size_ref,
             dst_ref=size_ref,
@@ -71,6 +71,17 @@
 class Copies:
     def __init__(self, send_sems, recv_sems):
         self.send_sems, self.recv_sems, self.all = send_sems, recv_sems, []
+
+    def join(self, flight, group):
+        for source, target, device in group:
+            pltpu.make_async_remote_copy(
+                src_ref=source,
+                dst_ref=target,
+                send_sem=self.send_sems.at[flight.index],
+                recv_sem=self.recv_sems.at[flight.index],
+                device_id=device,
+                device_id_type=MESH_ID,
+            ).start()
 
     def start(self, size_ref, group):
         index = len(self.all)
@@ -166,14 +177,22 @@
     )
     yield
     flight.wait_recv()
-    line = total.at[block, :, rows(at[second_axis] * tiny, tiny), :]
-    flight = copies.start(
-        total.at[block, :, pl.ds(0, 3 * tiny), :],
-        [(line, line, peer_on(second_axis, at, step)) for step in (1, 2, 3)],
+
+    def line_of(place):
+        return total.at[block, :, rows(lax.rem(place, 4) * tiny, tiny), :]
+
+    line = line_of(at[second_axis])
+    sides = copies.start(
+        total.at[block, :, pl.ds(0, 2 * tiny), :],
+        [(line, line, peer_on(second_axis, at, step)) for step in (1, 3)],
     )
+    across = copies.start(line, [(line, line, peer_on(second_axis, at, 2))])
+    flight = copies.start(total.at[block], [(line, line, sibling(at))])
     yield
-    flight.wait_recv()
-    flight = copies.start(total.at[block], [(total.at[block], total.at[block], sibling(at))])
+    sides.wait_recv()
+    copies.join(flight, [(line_of(at[second_axis] + step),) * 2 + (sibling(at),) for step in (1, 3)])
+    across.wait_recv()
+    copies.join(flight, [(line_of(at[second_axis] + 2),) * 2 + (sibling(at),)])
     yield
     flight.wait_recv()
     yield
@@ -195,11 +214,6 @@
         if index + 1 < count:
             rest = rest - piece.astype(F32)
     return pieces
-
-
-def column_of(row, size):
-    tall = jnp.transpose(jnp.broadcast_to(row, (128, size)))
-    return tall
 
 
 def unit_heads(values, width):
@@ -228,6 +242,7 @@
     ("target", (VARS, G_DEV), BF16),
     ("var", (1, VARS), F32),
     ("level", (1, 1), F32),
+    ("head_scale", (1, HEADS), F32),
 )
 
 SCRATCH = (
@@ -265,13 +280,13 @@
     ((ROWS, 3 * G_DEV), BF16),
     ((D, M_DEV), BF16),
     ((D, M_DEV), BF16),
+    ((2560, 128), F32),
     ((2048, 128), F32),
-    ((2048, 128), F32),
-    ((512, 128), F32),
+    ((D, 128), F32),
 )
 
 
-def step_kernel(head_scale_ref, *refs):
+def step_kernel(*refs):
     hbm, totals = refs[: len(INPUTS)], refs[len(INPUTS) : len(INPUTS) + len(TOTALS)]
     scratch = refs[len(INPUTS) + len(TOTALS) :]
     send_sems, recv_sems, load_sems = scratch[:3]
@@ -291,6 +306,7 @@
         target_ref,
         var_ref,
         level_ref,
+        head_scale_ref,
     ) = scratch[3 : 3 + len(INPUTS)]
     (
         state_in,
@@ -329,9 +345,9 @@
         head_grad,
         part_out,
         part_value,
-        part_dec,
+        gain_t,
     ) = scratch[3 + len(INPUTS) : 3 + len(INPUTS + SCRATCH)]
-    parts = (part_out, part_value, part_dec)
+    parts = (part_out, part_value)
     at = coordinates()
     band = at["band"]
     left = (lax.rem(band + 15, 16), at["x"], at["core"])
@@ -375,7 +391,7 @@
     loads["m2g"].wait()
     cell_flight = copies.start(m2g_in, [(m2g_ref, m2g_in.at[slot], device) for side, device, slot in sides])
     loads["target"].wait()
-    target_flights = [send_target(512 * chunk, 512) for chunk in range(3)]
+    target_flights = [send_target(512 * chunk, 512) for chunk in range(2)]
     loads["embed_in"].wait()
     pad_in[...] = jnp.zeros_like(pad_in)
     pad_in[:VARS, :] = embed_in_ref[...]
@@ -419,6 +435,8 @@
         weights_ref[:, block] = var_column * jnp.where(mine, lat_weight, 0.0)
 
     prepare(0, m2g_ref[...])
+    loads["gain"].wait()
+    gain_t[...] = jnp.transpose(jnp.broadcast_to(gain_ref[...], (128, D)))
     node_flight.wait_recv()
     for (first, size), flight in zip(CHUNKS, state_flights):
         cells = slice(first, first + size)
@@ -428,13 +446,12 @@
             encode(state_in[slot, :, cells], g2m_in[slot, :, cells])
 
     encoded = None
-    for piece in pieces_of(node_hidden[...], 3):
+    for piece in pieces_of(node_hidden[...], 2):
         term = dot(embed_out_t[...], piece)
         encoded = term if encoded is None else encoded + term
     mesh_in[...] = encoded
     mean_sq = jnp.mean(encoded * encoded, axis=0, keepdims=True)
-    loads["gain"].wait()
-    gain = lanes(column_of(gain_ref[...], D), M_DEV)
+    gain = lanes(gain_t[...], M_DEV)
     normed[...] = (encoded * lax.rsqrt(mean_sq + 1e-05) * gain).astype(BF16)
 
     normed_flights = []
@@ -450,13 +467,16 @@
             )
         )
 
-    target_flights.append(send_target(1536, 512))
+    target_flights += [send_target(512 * chunk, 512) for chunk in range(2, 4)]
 
     loads["qkv"].wait()
     q_t[...] = jnp.transpose(qkv_ref[0])
     k_t[...] = jnp.transpose(qkv_ref[1])
     v_t[...] = jnp.transpose(qkv_ref[2])
     unit_q[...] = unit_heads(dot(q_t[...], normed[...]), M_DEV).astype(BF16)
+
+    loads["head_scale"].wait()
+    score_scale = head_scale_ref[...] / HEAD_DIM
 
     def attend(near, start, width):
         keys = unit_heads(dot(k_t[...], near), width).astype(BF16)
@@ -467,7 +487,7 @@
         for head in range(HEADS):
             part = slice(HEAD_DIM * head, HEAD_DIM * head + HEAD_DIM)
             scores = dot(unit_k[start : start + width, part], unit_q[part, :])
-            exp = jnp.exp(scores * (head_scale_ref[head] / HEAD_DIM))
+            exp = jnp.exp(scores * score_scale[:, head : head + 1])
             exps[head, start : start + width, :] = exp
             sums_now.append(jnp.sum(exp * count, axis=0, keepdims=True))
         return sums_now
@@ -526,28 +546,32 @@
     mesh_out[...] = (mesh_in[...] + dot(out_t[...], attended[...])).astype(BF16)
     for index, piece in enumerate(pieces_of(dot(dec_t[:ROWS, :], mesh_out[...]), 2)):
         vars_two[ROWS * index : ROWS * index + ROWS, :] = piece
-    for flight in target_flights:
-        flight.wait_recv()
-
     scale_all = 1.0 / (MEMBERS * VARS)
     grad_scale = 2.0 * out_scale * scale_all
     grad_net[VARS:, :] = jnp.zeros((ROWS - VARS, 3 * G_DEV), BF16)
     loss_row = jnp.zeros((1, 512), F32)
     sources = ((noisy_ref, target_ref), (state_in.at[0], target_in.at[0]), (state_in.at[1], target_in.at[1]))
-    for place, (state, target) in enumerate(sources):
-        for chunk in range(4):
-            cells = slice(512 * chunk, 512 * chunk + 512)
-            block = slice(G_DEV * place + 512 * chunk, G_DEV * place + 512 * chunk + 512)
-            both = dot(vars_two[...], table[:, block])
-            net = both[:VARS, :] + both[ROWS : ROWS + VARS, :]
-            weights = weights_ref[:, block]
-            errors = skip_scale * state[:, cells].astype(F32) + out_scale * net - target[:, cells].astype(F32)
-            weighted = weights * errors
-            loss_row = loss_row + jnp.sum(weighted * errors, axis=0, keepdims=True)
-            grad_net[:VARS, block] = (grad_scale * weights * errors).astype(BF16)
+    chunks = [(0, chunk) for chunk in range(4)] + [(place, chunk) for chunk in range(4) for place in (1, 2)]
+    for place, chunk in chunks:
+        state, target = sources[place]
+        if place == 1 and chunk == 0:
+            target_flights[0].wait_recv()
+            target_flights[1].wait_recv()
+        if place == 1 and chunk == 2:
+            target_flights[2].wait_recv()
+            target_flights[3].wait_recv()
+        cells = slice(512 * chunk, 512 * chunk + 512)
+        block = slice(G_DEV * place + 512 * chunk, G_DEV * place + 512 * chunk + 512)
+        both = dot(vars_two[...], table[:, block])
+        net = both[:VARS, :] + both[ROWS : ROWS + VARS, :]
+        weights = weights_ref[:, block]
+        errors = skip_scale * state[:, cells].astype(F32) + out_scale * net - target[:, cells].astype(F32)
+        weighted = weights * errors
+        loss_row = loss_row + jnp.sum(weighted * errors, axis=0, keepdims=True)
+        grad_net[:VARS, block] = (grad_scale * weights * errors).astype(BF16)
     loss = jnp.sum(loss_row, axis=1, keepdims=True) * scale_all
     node_grad = dot_t(grad_net[...], table[...])
-    node_pieces = pieces_of(node_grad, 3)
+    node_pieces = pieces_of(node_grad, 2)
     grown = None
     for piece in node_pieces:
         term = dot(dec_full[:, :ROWS], piece)
@@ -560,37 +584,43 @@
         units.append(
             device_sum(parts[unit[0]], totals[unit[3]], unit, unit_refs[7 * index : 7 * index + 7], copies, at)
         )
-    out_units, value_units = (units[:4], units[4:])
+    out_units, value_units = (units[:3], units[3:])
     out_sum = dot_t(attended[...], mesh_grad[...])
     for lane in range(4):
         part_out[512 * lane : 512 * lane + 512, :] = out_sum[:, 128 * lane : 128 * lane + 128]
-    for unit in out_units[:3]:
+    for unit in out_units[:2]:
         next(unit)
     dec_sum = None
     for piece in node_pieces:
         term = dot_t(piece, mesh_out[...])
         dec_sum = term if dec_sum is None else dec_sum + term
     for lane in range(4):
-        part_dec[ROWS * lane : ROWS * lane + ROWS, :] = dec_sum[:, 128 * lane : 128 * lane + 128]
-    part_dec[4 * ROWS :, :] = jnp.broadcast_to(loss, (128, 128))
-    next(out_units[3])
+        start = 2048 + ROWS * lane
+        part_out[start : start + ROWS, :] = dec_sum[:, 128 * lane : 128 * lane + 128]
+    part_out[2048 + 4 * ROWS :, :] = jnp.broadcast_to(loss, (128, 128))
+    next(out_units[2])
     def advance(some):
         for unit in some:
             next(unit)
 
-    for head in range(HEADS):
-        part = slice(HEAD_DIM * head, HEAD_DIM * head + HEAD_DIM)
-        spread = dot_t(head_grad[part, :], probs[head]).astype(BF16)
-        part_value[512 * head : 512 * head + 512, :] = dot_t(normed[...], spread[:, :M_DEV]) + dot_t(
-            normed_in[...], spread[:, M_DEV:]
+    for pair in range(2):
+        spread = jnp.concatenate(
+            [
+                dot_t(head_grad[HEAD_DIM * head : HEAD_DIM * head + HEAD_DIM, :], probs[head]).astype(BF16)
+                for head in (2 * pair, 2 * pair + 1)
+            ],
+            axis=0,
         )
-        if head == 1:
+        both = dot_t(normed[...], spread[:, :M_DEV]) + dot_t(normed_in[...], spread[:, M_DEV:])
+        for index in range(2):
+            start = 1024 * pair + 512 * index
+            part_value[start : start + 512, :] = both[:, HEAD_DIM * index : HEAD_DIM * index + HEAD_DIM]
+        if pair == 0:
+            next(value_units[0])
             advance(out_units)
-        if head >= 1:
-            next(value_units[head - 1])
-        if head >= 2:
-            next(value_units[head - 2])
-    order = ((value_units[2:],),) + ((out_units, value_units),) * 6
+    advance(value_units[1:])
+    next(value_units[0])
+    order = ((value_units[1:],),) + ((out_units, value_units),) * 6
     for groups in order:
         for group in groups:
             advance(group)
@@ -599,23 +629,22 @@
         copy.wait_send()
 
 
-def finish_kernel(
-    out_a, out_b, value_a, value_b, dec_ref, out_hbm, value_hbm, dec_result, loss_result, sems
-):
+def finish_kernel(out_a, out_b, value_a, value_b, out_hbm, value_hbm, dec_result, loss_result, sems):
     flights = []
     for index, (source, tail, target) in enumerate(((out_a, out_b, out_hbm), (value_a, value_b, value_hbm))):
         for lane in range(4):
             flights.append(
                 pltpu.make_async_copy(
-                    source.at[pl.ds(512 * lane, 512), :] if lane < 3 else tail,
+                    source.at[pl.ds(512 * lane, 512), :] if lane < 3 else tail.at[pl.ds(0, 512), :],
                     target.at[:, pl.ds(128 * lane, 128)],
                     sems.at[4 * index + lane],
                 )
             )
             flights[-1].start()
     for lane in range(4):
-        dec_result[:, 128 * lane : 128 * lane + 128] = dec_ref[ROWS * lane : ROWS * lane + VARS, :]
-    loss_result[...] = dec_ref[4 * ROWS : 4 * ROWS + 1, :1] / GRID
+        start = 512 + ROWS * lane
+        dec_result[:, 128 * lane : 128 * lane + 128] = out_b[start : start + VARS, :]
+    loss_result[...] = out_b[512 + 4 * ROWS : 513 + 4 * ROWS, :1] / GRID
     for flight in flights:
         flight.wait()
 
@@ -637,9 +666,8 @@
     neighbours,
 ):
     vmem = pl.BlockSpec(memory_space=pltpu.VMEM)
-    smem = pl.BlockSpec(memory_space=pltpu.SMEM)
     anywhere = pl.BlockSpec(memory_space=pl.ANY)
-    copies = 15 + 7 * len(UNITS)
+    copies = 15 + 8 * len(UNITS)
     scratch = [pltpu.SemaphoreType.DMA((copies,))] * 2 + [pltpu.SemaphoreType.DMA((len(INPUTS),))]
     scratch += [pltpu.VMEM(entry[-2], entry[-1]) for entry in INPUTS + SCRATCH]
     for unit in UNITS:
@@ -647,7 +675,7 @@
     totals = pl.pallas_call(
         step_kernel,
         out_shape=[pltpu.VMEM(shape, F32) for shape in TOTALS],
-        in_specs=[smem] + [anywhere] * len(INPUTS),
+        in_specs=[anywhere] * len(INPUTS),
         out_specs=[vmem] * len(TOTALS),
         scratch_shapes=scratch,
         compiler_params=pltpu.CompilerParams(
@@ -655,7 +683,6 @@
         ),
         name="step",
     )(
-        head_scale,
         noisy_state,
         g2m_node.reshape(1, G_DEV),
         embed_in,
@@ -669,6 +696,7 @@
         target_state,
         var_weight.reshape(1, VARS),
         noise_level.reshape(1, 1),
+        head_scale.reshape(1, HEADS),
     )
     square = jax.ShapeDtypeStruct((D, D), F32)
     grad_out, grad_value, dec, loss = pl.pallas_call(

time: 78.3 us -> 76.9 us (0.982)
  Pallas kernels: 76.7 us -> 75.3 us
    pallas_call x1, Pallas kernels: 74.6 us -> 73.2 us  [local(): pl.pallas_call(step_kernel, out_shape=[pltpu.VMEM(shape, F32) for shape i...]
where the time goes in v4:
time: 76.9 us; the launch traced here: 76.8 us
  Pallas kernels  75.3 us (98%)
  between operations  1.47 us (2%)
    pallas_call x1, Pallas kernels, local(): pl.pallas_call(step_kernel, out_shape=[pltpu.VMEM(shape, F32) for shape i...  73.2 us
    pallas_call x1, Pallas kernels, local(): pl.pallas_call(finish_kernel, out_shape=(square, square, jax.ShapeDtypeSt...  2.05 us

profile of v4, /device:TPU:1, one launch (start us, length us, event | category | flops | bytes accessed | tf_op | source)
XLA Modules:
  0.0 76.8 jit_solution(15288865222965911494)
XLA Ops:
  1.3 73.2 %step.1 = (f32[4,4,96,128]{3,2,1,0:T(8,128)S(1)}, f32[2,4,128,128]{3,2,1,0:T(8,128)S(1)}, f32[4,4,96,128]{3,2,1,0:T(8,128)S(1)}, f32[2,4,64,128]{3,2,1,0:T(8,128)S(1)}) custom-call(bf16[1,84,2048]{2,1,0:T(8,128)(2,1)} %refs_0_.1, s32[1,2048]{1,0:T(1,128)} %bitcast.21, bf16[84,512]{1,0:T(8,128)(2,1)} %refs_2_.1, bf16[512,512]{1,0:T(8,128)(2,1)} %refs_3_.1, ...), custom_call_target="tpu_custom_call" | custom-call | tf_op jit(solution)/shard_map/step/pallas_call | solution.py:675
  74.5 2.1 %finish.1 = (f32[512,512]{1,0:T(8,128)}, f32[512,512]{1,0:T(8,128)}, f32[84,512]{1,0:T(8,128)}, f32[1,1]{1,0:T(1,128)}) custom-call(f32[1536,128]{1,0:T(8,128)S(1)} %bitcast.15, f32[1024,128]{1,0:T(8,128)S(1)} %bitcast.17, f32[1536,128]{1,0:T(8,128)S(1)} %bitcast.16, f32[512,128]{1,0:T(8,128)S(1)} %bitcast.18), custom_call_target="tpu_custom_call" | custom-call | tf_op jit(solution)/shard_map/finish/pallas_call | solution.py:702

commit v5 on v4

--- a/solution.py
+++ b/solution.py
@@ -226,7 +226,7 @@
     return jnp.concatenate([values] * (width // 128), axis=1)
 
 
-STEP_VMEM = 59 << 20
+STEP_VMEM = 61 << 20
 CHUNKS = ((0, 512), (512, 512), (1024, 512), (1536, 256), (1792, 256))
 INPUTS = (
     ("noisy", (VARS, G_DEV), BF16),
@@ -283,6 +283,7 @@
     ((2560, 128), F32),
     ((2048, 128), F32),
     ((D, 128), F32),
+    ((3 * G_DEV, M_DEV), BF16),
 )
 
 
@@ -346,6 +347,7 @@
         part_out,
         part_value,
         gain_t,
+        table_t,
     ) = scratch[3 + len(INPUTS) : 3 + len(INPUTS + SCRATCH)]
     parts = (part_out, part_value)
     at = coordinates()
@@ -429,6 +431,10 @@
         ids = lax.broadcasted_iota(I32, (M_DEV, G_DEV), 0)
         block = slice(G_DEV * place, G_DEV * place + G_DEV)
         table[:, block] = jnp.where(local == ids, 1.0, 0.0).astype(BF16)
+        upright = jnp.transpose(jnp.broadcast_to(local.astype(F32), (128, G_DEV))).astype(I32)
+        for lane in range(4):
+            ids = lax.broadcasted_iota(I32, (G_DEV, 128), 1) + 128 * lane
+            table_t[block, 128 * lane : 128 * lane + 128] = jnp.where(upright == ids, 1.0, 0.0).astype(BF16)
         cells = lax.broadcasted_iota(I32, (1, G_DEV), 1) + lax.rem(band + (0, 15, 1)[place], 16) * G_DEV
         lat_weight = 0.2 + jnp.cos(math.pi * (cells.astype(F32) + 0.5) / GRID - 0.5 * math.pi)
         mine = (local >= 0) & (local < M_DEV)
@@ -570,14 +576,13 @@
         loss_row = loss_row + jnp.sum(weighted * errors, axis=0, keepdims=True)
         grad_net[:VARS, block] = (grad_scale * weights * errors).astype(BF16)
     loss = jnp.sum(loss_row, axis=1, keepdims=True) * scale_all
-    node_grad = dot_t(grad_net[...], table[...])
+    node_grad = dot(grad_net[...], table_t[...])
     node_pieces = pieces_of(node_grad, 2)
     grown = None
     for piece in node_pieces:
         term = dot(dec_full[:, :ROWS], piece)
         grown = term if grown is None else grown + term
     mesh_grad[...] = grown.astype(BF16)
-    head_grad[...] = dot(out_w_ref[...], mesh_grad[...]).astype(BF16)
 
     units = []
     for index, unit in enumerate(UNITS):
@@ -590,6 +595,7 @@
         part_out[512 * lane : 512 * lane + 512, :] = out_sum[:, 128 * lane : 128 * lane + 128]
     for unit in out_units[:2]:
         next(unit)
+    head_grad[...] = dot(out_w_ref[...], mesh_grad[...]).astype(BF16)
     dec_sum = None
     for piece in node_pieces:
         term = dot_t(piece, mesh_out[...])

time: 76.9 us -> 76.2 us (level)
  no operation moved by 1% of the time
where the time goes in v5:
time: 76.2 us; the launch traced here: 76.1 us
  Pallas kernels  74.7 us (98%)
  between operations  1.47 us (2%)
    pallas_call x1, Pallas kernels, local(): pl.pallas_call(step_kernel, out_shape=[pltpu.VMEM(shape, F32) for shape i...  72.6 us
    pallas_call x1, Pallas kernels, local(): pl.pallas_call(finish_kernel, out_shape=(square, square, jax.ShapeDtypeSt...  2.05 us

profile of v5, /device:TPU:1, one launch (start us, length us, event | category | flops | bytes accessed | tf_op | source)
XLA Modules:
  0.0 76.1 jit_solution(7453244843032561800)
XLA Ops:
  1.3 72.6 %step.1 = (f32[4,4,96,128]{3,2,1,0:T(8,128)S(1)}, f32[2,4,128,128]{3,2,1,0:T(8,128)S(1)}, f32[4,4,96,128]{3,2,1,0:T(8,128)S(1)}, f32[2,4,64,128]{3,2,1,0:T(8,128)S(1)}) custom-call(bf16[1,84,2048]{2,1,0:T(8,128)(2,1)} %refs_0_.1, s32[1,2048]{1,0:T(1,128)} %bitcast.21, bf16[84,512]{1,0:T(8,128)(2,1)} %refs_2_.1, bf16[512,512]{1,0:T(8,128)(2,1)} %refs_3_.1, ...), custom_call_target="tpu_custom_call" | custom-call | tf_op jit(solution)/shard_map/step/pallas_call | solution.py:681
  73.9 2.1 %finish.1 = (f32[512,512]{1,0:T(8,128)}, f32[512,512]{1,0:T(8,128)}, f32[84,512]{1,0:T(8,128)}, f32[1,1]{1,0:T(1,128)}) custom-call(f32[1536,128]{1,0:T(8,128)S(1)} %bitcast.15, f32[1024,128]{1,0:T(8,128)S(1)} %bitcast.17, f32[1536,128]{1,0:T(8,128)S(1)} %bitcast.16, f32[512,128]{1,0:T(8,128)S(1)} %bitcast.18), custom_call_target="tpu_custom_call" | custom-call | tf_op jit(solution)/shard_map/finish/pallas_call | solution.py:708
